TPU v7x, 32 devices: a whole 2x2x4 slice. The times are simulated.
32 devices in a mesh: grp: 2 (over y), mem: 16 (over z, x, core).
Axes of the slice: x: 2, y: 2, z: 4, core: 2. Of those that a mesh axis runs over, the one named last changes fastest.
Arguments:
- tokens: bfloat16 [4096, 1024], P(('grp', 'mem')), may hold values from -6 to 6
- cotangent: bfloat16 [4096, 1024], P(('grp', 'mem')), may hold values from -6 to 6
- path: int32 [32, 3], P(('grp', 'mem')), may hold values from 0 to 63, as said below
- coarse_weights: bfloat16 [4, 1024, 512], P(None, 'mem'), may hold values from -0.1875 to 0.1875
- middle_weights: bfloat16 [64, 1024, 256], P(None, 'mem'), may hold values from -0.1875 to 0.1875
- fine_weights: bfloat16 [64, 1024, 128], P('grp', 'mem'), may hold values from -0.1875 to 0.1875
Outputs:
- tokens_grad: bfloat16 [4096, 1024], P(('grp', 'mem'))
- coarse_grad: bfloat16 [4, 1024, 512], P(None, 'mem')
- middle_grad: bfloat16 [64, 1024, 256], P(None, 'mem')
- fine_grad: bfloat16 [64, 1024, 128], P('grp', 'mem')
Inputs may be any that keep to these rules, and one draw needn't show every extreme that they name: Row d is the path of document d: column 0 its coarse block, column 1 its middle block, column 2 its fine block, with middle = fine * 1 and coarse = middle * 4 // 64. Some fine blocks are chosen by many documents.
All inputs are finite; a program needn't handle non-finite values.
Results may differ from a plain program's by a relative error of at most 0.005.
Values may be sent and summed in bfloat16 or wider, within the bound.
A program may use at most 64 MiB of HBM per device.

v0:
```python
import functools
import math

import jax
import jax.numpy as jnp
from jax import lax
from jax.experimental import pallas as pl
from jax.experimental.pallas import tpu as pltpu
from jax.sharding import PartitionSpec as P

MESH = pl.DeviceIdType.MESH
LANES = 128
F32 = jnp.float32
BF16 = jnp.bfloat16


def gelu_parts(before, hidden_grad):
    scale = math.sqrt(2.0 / math.pi)
    square = before * before
    tanh = jnp.tanh(scale * (before + 0.044715 * (square * before)))
    half = 0.5 * (1.0 + tanh)
    hidden = before * half
    slope = half + 0.5 * before * (1.0 - tanh * tanh) * (scale * (1.0 + 3 * 0.044715 * square))
    return hidden.astype(BF16), (hidden_grad * slope).astype(BF16)


def dot(left, right):
    return jnp.dot(left, right, preferred_element_type=F32)


def dot_transposed(left, right):
    return lax.dot_general(left, right, (((1,), (1,)), ((), ())), preferred_element_type=F32)


def level(weights, x, g, xt, gt):
    width = weights.shape[1]
    half = width // 2
    if half % LANES == 0:
        up = weights[:, :half]
        down = weights[:, half:]
        hidden, grad = gelu_parts(dot(x, up), dot(g, down))
        term = jnp.concatenate(
            [dot(xt, grad).astype(BF16), dot(gt, hidden).astype(BF16)], axis=1
        )
        return term, dot_transposed(grad, up)
    before = dot(x, weights)
    hidden_grad = pltpu.roll(dot(g, weights), half, 1)
    hidden, grad = gelu_parts(before, hidden_grad)
    first = lax.broadcasted_iota(jnp.int32, grad.shape, 1) < half
    grad = jnp.where(first, grad.astype(F32), 0.0).astype(BF16)
    hidden = jnp.where(first, hidden.astype(F32), 0.0)
    hidden = pltpu.roll(hidden, half, 1).astype(BF16)
    term = (dot(xt, grad) + dot(gt, hidden)).astype(BF16)
    return term, dot_transposed(grad, weights)


def plan(groups, members, blocks_width):
    inner = max(k for k in range(1, math.isqrt(members) + 1) if members % k == 0)
    team = math.gcd(groups, blocks_width // LANES)
    return members // inner, inner, team


def main_kernel(
    groups,
    members,
    path_row,
    tokens_hbm,
    cotangent_hbm,
    coarse_hbm,
    middle_hbm,
    fine_hbm,
    all_paths,
    tokens_grad,
    middle_parts,
    fine_parts,
    coarse_parts,
    path,
    tokens,
    cotangent,
    coarse_w,
    middle_w,
    fine_w,
    middle_send,
    fine_out,
    fine_in,
    fine_send,
    coarse_line,
    coarse_send,
    coarse_block,
    middle_block,
    fine_block,
    coarse_term,
    middle_term,
    fine_term,
    coarse_terms_in,
    coarse_sums,
    coarse_sums_in,
    coarse_total,
    xt,
    gt,
    total,
    path_send,
    path_recv,
    mem_send,
    mem_recv,
    grp_send,
    grp_recv,
    line_send,
    line_recv,
    team_send,
    team_recv,
    local_sem,
    load_sem,
    middle_send_on,
    middle_recv_on,
    fine_send_on,
    fine_recv_on,
):
    group = lax.axis_index("grp")
    me = lax.axis_index("mem")
    count = groups * members
    device = group * members + me
    owned = fine_w.shape[0]
    coarse_count, rows, wide = coarse_w.shape
    outer, inner, team = plan(groups, members, wide)
    size = team * inner
    columns = wide // team
    line = me // inner
    place = lax.rem(me, inner)
    slot = lax.rem(group, team)
    team_first = group - slot
    spot = slot * inner + place

    def loop(start, stop, body):
        def wrapped(step, carry):
            body(step)
            return carry

        lax.fori_loop(start, stop, wrapped, 0)

    def column_range(s):
        return pl.ds(pl.multiple_of(s * columns, LANES), columns)

    loads = [
        pltpu.make_async_copy(source, target, load_sem.at[index])
        for index, (source, target) in enumerate(
            (
                (coarse_hbm, coarse_w),
                (fine_hbm, fine_w),
                (middle_hbm, middle_w),
                (tokens_hbm, tokens),
                (cotangent_hbm, cotangent),
            )
        )
    ]
    for load in loads:
        load.start()
    barrier = pltpu.get_barrier_semaphore()

    def anyone(step):
        other = lax.rem(device + step, count)
        return other, (other // members, lax.rem(other, members))

    def greet(step):
        _, where = anyone(step)
        pl.semaphore_signal(barrier, inc=1, device_id=where, device_id_type=MESH)

    loop(1, count, greet)
    own_columns = coarse_w.at[:, :, column_range(slot)]
    loads[0].wait()
    line_self = pltpu.make_async_copy(own_columns, coarse_line.at[line], local_sem.at[0])
    line_self.start()
    pl.semaphore_wait(barrier, count - 1)

    def path_copy(step, landing_own):
        other, where = anyone(step)
        return pltpu.make_async_remote_copy(
            src_ref=path_row,
            dst_ref=all_paths.at[device if landing_own else other],
            send_sem=path_send.at[other],
            recv_sem=path_recv.at[device if landing_own else other],
            device_id=where,
            device_id_type=MESH,
        )

    loop(1, count, lambda step: path_copy(step, True).start())
    all_paths[device] = path_row[...]

    def line_copy(index, source, target, step, landing_own):
        other = lax.rem(line + step, outer)
        landing = line if landing_own else other
        return pltpu.make_async_remote_copy(
            src_ref=source(other),
            dst_ref=target.at[landing],
            send_sem=line_send.at[index, other],
            recv_sem=line_recv.at[index, landing],
            device_id={"mem": other * inner + place},
            device_id_type=MESH,
        )

    first_stage = (0, lambda other: own_columns, coarse_line)
    loop(1, outer, lambda step: line_copy(*first_stage, step, True).start())

    for load in loads[1:]:
        load.wait()
    width = tokens.shape[1]
    for start in range(0, width, LANES):
        part = slice(start, start + LANES)
        xt[part, :] = tokens[:, part].T
        gt[part, :] = cotangent[:, part].T

    def path_done(step):
        done = path_copy(step, False)
        done.wait_recv()
        done.wait_send()

    loop(1, count, path_done)
    scalars = pltpu.make_async_copy(all_paths, path, local_sem.at[1])
    scalars.start()
    scalars.wait()

    def route(document, column):
        return path[document, 0, column]

    def member_copy(index, source, target, p, landing_own):
        landing = me if landing_own else p
        return pltpu.make_async_remote_copy(
            src_ref=source.at[p],
            dst_ref=target.at[landing],
            send_sem=mem_send.at[index, p],
            recv_sem=mem_recv.at[index, landing],
            device_id={"mem": p},
            device_id_type=MESH,
        )

    def spread(index, source, target):
        loop(
            1,
            members,
            lambda step: member_copy(
                index, source, target, lax.rem(me + step, members), True
            ).start(),
        )

    def arrive(index, source, target):
        loop(
            1,
            members,
            lambda step: member_copy(
                index, source, target, lax.rem(me + members - step, members), False
            ).wait_recv(),
        )

    def left(index, source, target):
        loop(
            1,
            members,
            lambda step: member_copy(
                index, source, target, lax.rem(me + step, members), False
            ).wait_send(),
        )

    def group_copy(index, source, target, step, landing_own):
        other = lax.rem(group + step, groups)
        landing = group if landing_own else other
        return pltpu.make_async_remote_copy(
            src_ref=source(other),
            dst_ref=target.at[landing],
            send_sem=grp_send.at[index, other],
            recv_sem=grp_recv.at[index, landing],
            device_id={"grp": other},
            device_id_type=MESH,
        )

    def group_spread(*what):
        loop(1, groups, lambda step: group_copy(*what, step, True).start())

    def group_arrive(*what):
        loop(1, groups, lambda step: group_copy(*what, step, False).wait_recv())

    def group_left(*what):
        loop(1, groups, lambda step: group_copy(*what, step, False).wait_send())

    def team_copy(index, source, target, step, landing_own):
        other = lax.rem(spot + step, size)
        landing = spot if landing_own else other
        return pltpu.make_async_remote_copy(
            src_ref=source(other),
            dst_ref=target(landing),
            send_sem=team_send.at[index, other],
            recv_sem=team_recv.at[index, landing],
            device_id=(team_first + other // inner, line * inner + lax.rem(other, inner)),
            device_id_type=MESH,
        )

    def team_document(t):
        return (team_first + t // inner) * members + line * inner + lax.rem(t, inner)

    def pick_fine(index):
        held = jnp.clip(route(index, 2) - group * owned, 0, owned - 1)
        fine_out[index // members, lax.rem(index, members)] = fine_w[held]

    def pick_middle(p):
        middle_send[p] = middle_w[route(group * members + p, 1)]

    loop(0, count, pick_fine)
    fine_trade = (0, lambda other: fine_out.at[other], fine_in)
    group_spread(*fine_trade)
    loop(0, members, pick_middle)
    spread(0, middle_send, middle_block)
    fine_in[group] = fine_out[group]
    middle_block[me] = middle_send[me]

    def merge_fine(p):
        owner = route(group * members + p, 2) // owned
        fine_send[p] = fine_in[owner, p]

    group_arrive(*fine_trade)
    loop(0, members, merge_fine)
    spread(1, fine_send, fine_block)
    fine_block[me] = fine_send[me]

    line_self.wait()
    loop(1, outer, lambda step: line_copy(*first_stage, step, False).wait_recv())

    def pick_coarse(t):
        identity = route(team_document(t), 0)
        for z in range(outer):
            coarse_send[t, z] = coarse_line[z, identity]

    loop(0, size, pick_coarse)

    def piece_of(ref, t, s):
        return ref.at[:, lax.rem(t, inner), :, column_range(s)]

    second_stage = (
        0,
        lambda other: coarse_send.at[other],
        lambda landing: piece_of(coarse_block, landing, landing // inner),
    )
    loop(1, size, lambda step: team_copy(*second_stage, step, True).start())
    block_self = pltpu.make_async_copy(
        coarse_send.at[spot], piece_of(coarse_block, place, slot), local_sem.at[2]
    )
    block_self.start()

    def compute(block, term):
        weights = block[...].reshape(width, block.shape[-1])
        value, part = level(weights, tokens[...], cotangent[...], xt[...], gt[...])
        term[...] = value.reshape(term.shape)
        return part

    middle_own = middle_parts.at[group]
    fine_own = fine_parts.at[group]

    arrive(0, middle_send, middle_block)
    total[...] = compute(middle_block, middle_term)
    spread(2, middle_term, middle_own)
    middle_parts[group, me] = middle_term[me]

    loop(1, size, lambda step: team_copy(*second_stage, step, False).wait_recv())
    block_self.wait()
    total[...] += compute(coarse_block, coarse_term)
    gather_terms = (
        1,
        lambda other: piece_of(coarse_term, other, other // inner),
        lambda landing: coarse_terms_in.at[landing],
    )
    loop(1, size, lambda step: team_copy(*gather_terms, step, True).start())
    term_self = pltpu.make_async_copy(
        piece_of(coarse_term, place, slot), coarse_terms_in.at[spot], local_sem.at[3]
    )
    term_self.start()

    arrive(1, fine_send, fine_block)
    part = compute(fine_block, fine_term)
    spread(3, fine_term, fine_own)
    fine_parts[group, me] = fine_term[me]
    tokens_grad[...] = (total[...] + part).astype(BF16)

    def hand_on(target, send_on, recv_on, p, step, landing_own):
        other = lax.rem(group + step, groups)
        landing = group if landing_own else other
        return pltpu.make_async_remote_copy(
            src_ref=target.at[group, p],
            dst_ref=target.at[landing, p],
            send_sem=send_on.at[other, p],
            recv_sem=recv_on.at[landing, p],
            device_id={"grp": other},
            device_id_type=MESH,
        )

    def relay(index, source, target, send_on, recv_on):
        own = target.at[group]

        def start(p):
            loop(1, groups, lambda step: hand_on(target, send_on, recv_on, p, step, True).start())

        def body(step):
            p = lax.rem(me + members - step, members)
            member_copy(index, source, own, p, False).wait_recv()
            start(p)

        start(me)
        loop(1, members, body)

    def relay_done(target, send_on, recv_on):
        def body(index):
            p = index // (groups - 1)
            step = lax.rem(index, groups - 1) + 1
            done = hand_on(target, send_on, recv_on, p, step, False)
            done.wait_recv()
            done.wait_send()

        if groups > 1:
            loop(0, members * (groups - 1), body)

    relay(2, middle_term, middle_parts, middle_send_on, middle_recv_on)

    loop(1, size, lambda step: team_copy(*gather_terms, step, False).wait_recv())
    term_self.wait()
    step_rows = min(rows, 16)
    weight = [
        [jnp.where(route(team_document(t), 0) == k, 1.0, 0.0) for k in range(coarse_count)]
        for t in range(size)
    ]

    def add_terms(index):
        z = index // (rows // step_rows)
        some = pl.ds(pl.multiple_of(lax.rem(index, rows // step_rows) * step_rows, step_rows), step_rows)
        pieces = [coarse_terms_in[t, z, some, :].astype(F32) for t in range(size)]
        for k in range(coarse_count):
            value = pieces[0] * weight[0][k]
            for t in range(1, size):
                value = value + pieces[t] * weight[t][k]
            coarse_sums[z, k, some, :] = value.astype(BF16)

    loop(0, outer * (rows // step_rows), add_terms)
    sum_stage = (1, lambda other: coarse_sums.at[other], coarse_sums_in)
    loop(1, outer, lambda step: line_copy(*sum_stage, step, True).start())
    coarse_sums_in[line] = coarse_sums[line]
    relay(3, fine_term, fine_parts, fine_send_on, fine_recv_on)


    left(0, middle_send, middle_block)
    left(1, fine_send, fine_block)
    group_left(*fine_trade)
    loop(1, outer, lambda step: line_copy(*first_stage, step, False).wait_send())
    loop(1, size, lambda step: team_copy(*second_stage, step, False).wait_send())
    loop(1, size, lambda step: team_copy(*gather_terms, step, False).wait_send())
    left(2, middle_term, middle_own)
    left(3, fine_term, fine_own)

    loop(1, outer, lambda step: line_copy(*sum_stage, step, False).wait_recv())
    value = coarse_sums_in[0].astype(F32)
    for z in range(1, outer):
        value = value + coarse_sums_in[z].astype(F32)
    coarse_total[...] = value.astype(BF16)
    coarse_trade = (1, lambda other: coarse_total, coarse_parts)
    group_spread(*coarse_trade)
    coarse_parts[group] = coarse_total[...]
    loop(1, outer, lambda step: line_copy(*sum_stage, step, False).wait_send())
    group_arrive(*coarse_trade)
    group_left(*coarse_trade)
    relay_done(middle_parts, middle_send_on, middle_recv_on)
    relay_done(fine_parts, fine_send_on, fine_recv_on)


def exchange(path, tokens, cotangent, coarse_w, middle_w, fine_w, groups, members):
    blocks, rows, wide = coarse_w.shape
    medium, narrow = middle_w.shape[2], fine_w.shape[2]
    token_count, width = tokens.shape
    count = groups * members
    outer, inner, team = plan(groups, members, wide)
    columns = wide // team
    size = team * inner

    def stack(*shape):
        return pltpu.VMEM(shape, BF16)

    def sems(*shape):
        return pltpu.SemaphoreType.DMA(shape)

    vmem = pl.BlockSpec(memory_space=pltpu.VMEM)
    return pl.pallas_call(
        functools.partial(main_kernel, groups, members),
        out_shape=(
            jax.ShapeDtypeStruct((count,) + path.shape, jnp.int32),
            jax.ShapeDtypeStruct(tokens.shape, BF16),
            jax.ShapeDtypeStruct((groups, members, rows, medium), BF16),
            jax.ShapeDtypeStruct((groups, members, rows, narrow), BF16),
            jax.ShapeDtypeStruct((groups, blocks, rows, columns), BF16),
        ),
        in_specs=[vmem] + [pl.BlockSpec(memory_space=pl.ANY)] * 5,
        out_specs=(vmem,) * 5,
        scratch_shapes=[
            pltpu.SMEM((count,) + path.shape, jnp.int32),
            stack(*tokens.shape),
            stack(*cotangent.shape),
            stack(*coarse_w.shape),
            stack(*middle_w.shape),
            stack(*fine_w.shape),
            stack(members, rows, medium),
            stack(groups, members, rows, narrow),
            stack(groups, members, rows, narrow),
            stack(members, rows, narrow),
            stack(outer, blocks, rows, columns),
            stack(size, outer, rows, columns),
            stack(outer, inner, rows, wide),
            stack(members, rows, medium),
            stack(members, rows, narrow),
            stack(outer, inner, rows, wide),
            stack(members, rows, medium),
            stack(members, rows, narrow),
            stack(size, outer, rows, columns),
            stack(outer, blocks, rows, columns),
            stack(outer, blocks, rows, columns),
            stack(blocks, rows, columns),
            stack(width, token_count),
            stack(width, token_count),
            pltpu.VMEM((token_count, width), F32),
            sems(count),
            sems(count),
            sems(4, members),
            sems(4, members),
            sems(2, groups),
            sems(2, groups),
            sems(2, outer),
            sems(2, outer),
            sems(2, size),
            sems(2, size),
            sems(4),
            sems(5),
            sems(groups, members),
            sems(groups, members),
            sems(groups, members),
            sems(groups, members),
        ],
        compiler_params=pltpu.CompilerParams(
            collective_id=0, has_side_effects=True, vmem_limit_bytes=60 * 2**20
        ),
        name="exchange",
    )(path, tokens, cotangent, coarse_w, middle_w, fine_w)


def collect_kernel(
    path,
    first_owned,
    tokens_in,
    middle_hbm,
    fine_hbm,
    coarse_parts,
    tokens_grad,
    coarse_grad,
    middle_grad,
    fine_grad,
    middle_parts,
    fine_parts,
    middle_sum,
    fine_sum,
    middle_last,
    fine_last,
    load_sem,
):
    count = middle_parts.shape[0]
    owned = fine_grad.shape[0]
    loads = (
        pltpu.make_async_copy(middle_hbm, middle_parts, load_sem.at[0]),
        pltpu.make_async_copy(fine_hbm, fine_parts, load_sem.at[1]),
    )
    for load in loads:
        load.start()
    middle_grad[...] = jnp.zeros_like(middle_grad)
    fine_grad[...] = jnp.zeros_like(fine_grad)
    middle_sum[count] = jnp.zeros(middle_sum.shape[1:], F32)
    fine_sum[count] = jnp.zeros(fine_sum.shape[1:], F32)
    for last in (middle_last, fine_last):

        def clear(k, carry, last=last):
            last[k] = count
            return carry

        lax.fori_loop(0, last.shape[0], clear, 0)
    tokens_grad[...] = tokens_in[...]
    groups, _, _, columns = coarse_parts.shape
    team = coarse_grad.shape[2] // columns
    for s in range(team):
        value = coarse_parts[s].astype(F32)
        for other in range(s + team, groups, team):
            value = value + coarse_parts[other].astype(F32)
        coarse_grad[:, :, s * columns : (s + 1) * columns] = value.astype(BF16)
    for load in loads:
        load.wait()

    def add(document, carry):
        k = path[document, 0, 1]
        value = middle_parts[document].astype(F32) + middle_sum[middle_last[k]]
        middle_sum[document] = value
        middle_grad[k] = value.astype(BF16)
        middle_last[k] = document
        place = path[document, 0, 2] - first_owned[0]

        @pl.when((place >= 0) & (place < owned))
        def _():
            piece = fine_parts[document].astype(F32) + fine_sum[fine_last[place]]
            fine_sum[document] = piece
            fine_grad[place] = piece.astype(BF16)
            fine_last[place] = document

        return carry

    lax.fori_loop(0, count, add, 0)


def collect(paths, first_owned, tokens_grad, middle_parts, fine_parts, coarse_parts, shapes):
    vmem = pl.BlockSpec(memory_space=pltpu.VMEM)
    smem = pl.BlockSpec(memory_space=pltpu.SMEM)
    hbm = pl.BlockSpec(memory_space=pl.ANY)
    count, rows, medium = middle_parts.shape
    narrow = fine_parts.shape[2]
    return pl.pallas_call(
        collect_kernel,
        out_shape=tuple(
            jax.ShapeDtypeStruct(shape, BF16) for shape in (tokens_grad.shape,) + shapes
        ),
        in_specs=[smem, smem, vmem, hbm, hbm, vmem],
        out_specs=(vmem,) * 4,
        scratch_shapes=[
            pltpu.VMEM(middle_parts.shape, BF16),
            pltpu.VMEM(fine_parts.shape, BF16),
            pltpu.VMEM((count + 1, rows, medium), F32),
            pltpu.VMEM((count + 1, rows, narrow), F32),
            pltpu.SMEM((shapes[1][0],), jnp.int32),
            pltpu.SMEM((shapes[2][0],), jnp.int32),
            pltpu.SemaphoreType.DMA((2,)),
        ],
        compiler_params=pltpu.CompilerParams(vmem_limit_bytes=60 * 2**20),
        name="collect",
    )(paths, first_owned, tokens_grad, middle_parts, fine_parts, coarse_parts)


def on_device(tokens, cotangent, path, coarse_weights, middle_weights, fine_weights):
    members = lax.axis_size("mem")
    groups = lax.axis_size("grp")
    paths, tokens_grad, middle_parts, fine_parts, coarse_parts = exchange(
        path, tokens, cotangent, coarse_weights, middle_weights, fine_weights, groups, members
    )
    first_owned = (lax.axis_index("grp") * fine_weights.shape[0]).astype(jnp.int32).reshape(1)
    flat = lambda parts: parts.reshape((groups * members,) + parts.shape[2:])
    return collect(
        paths,
        first_owned,
        tokens_grad,
        flat(middle_parts),
        flat(fine_parts),
        coarse_parts,
        (coarse_weights.shape, middle_weights.shape, fine_weights.shape),
    )


def solution(mesh):
    return jax.shard_map(
        on_device,
        mesh=mesh,
        in_specs=(
            P(("grp", "mem"), None),
            P(("grp", "mem"), None),
            P(("grp", "mem"), None),
            P(None, "mem", None),
            P(None, "mem", None),
            P("grp", "mem", None),
        ),
        out_specs=(
            P(("grp", "mem"), None),
            P(None, "mem", None),
            P(None, "mem", None),
            P("grp", "mem", None),
        ),
        check_vma=False,
    )
```

profile of v0, /device:TPU:11, one launch (start us, length us, event | category | flops | bytes accessed | tf_op | source)
XLA Modules:
  0.0 87.6 jit_solution(14254881850600471613)
XLA Ops:
  0.6 82.1 %exchange.1 = (s32[32,1,3]{2,1,0:T(1,128)}, bf16[128,1024]{1,0:T(8,128)(2,1)}, bf16[2,16,64,256]{3,2,1,0:T(8,128)(2,1)}, bf16[2,16,64,128]{3,2,1,0:T(8,128)(2,1)}, bf16[2,4,64,256]{3,2,1,0:T(8,128)(2,1)}) custom-call(s32[1,3]{1,0:T(1,128)} %path_row.1, bf16[128,1024]{1,0:T(8,128)(2,1)} %tokens_hbm.1, bf16[128,1024]{1,0:T(8,128)(2,1)} %cotangent_hbm.1, ...), custom_call_target="tpu_custom_call" | custom-call | tf_op jit(solution)/shard_map/exchange/pallas_call | solution.py:485
  82.7 4.9 %collect.1 = (bf16[128,1024]{1,0:T(8,128)(2,1)}, bf16[4,64,512]{2,1,0:T(8,128)(2,1)}, bf16[64,64,256]{2,1,0:T(8,128)(2,1)}, bf16[32,64,128]{2,1,0:T(8,128)(2,1)}) custom-call(s32[32,1,3]{2,1,0:T(1,128)} %get-tuple-element.9.path, s32[1]{0:T(128)} %bitcast.first_owned, bf16[128,1024]{1,0:T(8,128)(2,1)} %get-tuple-element.10.tokens_in, ...), custom_call_target="tpu_custom_call" | custom-call | tf_op jit(solution)/shard_map/collect/pallas_call | solution.py:621
where the time goes:
time: 87.8 us; the launch traced here: 87.6 us
  Pallas kernels  86.9 us (99%)
    pallas_call x1, Pallas kernels, exchange(): pl.pallas_call(functools.partial(main_kernel, groups, members), out_shape...  82.1 us
    pallas_call x1, Pallas kernels, collect(): pl.pallas_call(collect_kernel, out_shape=tuple((jax.ShapeDtypeStruct(shap...  4.88 us

commit v1 on v0

--- a/solution.py
+++ b/solution.py
@@ -56,8 +56,16 @@
 
 def plan(groups, members, blocks_width):
     inner = max(k for k in range(1, math.isqrt(members) + 1) if members % k == 0)
-    team = math.gcd(groups, blocks_width // LANES)
-    return members // inner, inner, team
+    cores = 2 if inner % 2 == 0 else 1
+    return members // inner, inner // cores, cores
+
+
+def bits_of(outer):
+    bits = []
+    while outer > 1:
+        outer //= 2
+        bits.append(outer)
+    return bits
 
 
 def main_kernel(
@@ -75,8 +83,8 @@
     fine_parts,
     coarse_parts,
     path,
-    tokens,
-    cotangent,
+    both,
+    other_doc,
     coarse_w,
     middle_w,
     fine_w,
@@ -84,31 +92,40 @@
     fine_out,
     fine_in,
     fine_send,
-    coarse_line,
-    coarse_send,
-    coarse_block,
     middle_block,
     fine_block,
-    coarse_term,
     middle_term,
     fine_term,
-    coarse_terms_in,
-    coarse_sums,
-    coarse_sums_in,
+    sums,
+    from_core,
+    from_side,
+    from_line,
     coarse_total,
-    xt,
-    gt,
+    flipped,
+    pair_t,
     total,
+    pre_give,
+    pre_take,
+    act_give,
+    act_take,
+    back_give,
+    back_take,
     path_send,
     path_recv,
     mem_send,
     mem_recv,
     grp_send,
     grp_recv,
-    line_send,
-    line_recv,
-    team_send,
-    team_recv,
+    pair_send,
+    pair_recv,
+    gather_send,
+    gather_recv,
+    side_send,
+    side_recv,
+    core_send,
+    core_recv,
+    fold_send,
+    fold_recv,
     local_sem,
     load_sem,
     middle_send_on,
@@ -121,15 +138,16 @@
     count = groups * members
     device = group * members + me
     owned = fine_w.shape[0]
-    coarse_count, rows, wide = coarse_w.shape
-    outer, inner, team = plan(groups, members, wide)
-    size = team * inner
-    columns = wide // team
+    blocks, outer, sides, cores, rows, columns = coarse_w.shape
+    inner = sides * cores
+    bits = bits_of(outer)
     line = me // inner
     place = lax.rem(me, inner)
-    slot = lax.rem(group, team)
-    team_first = group - slot
-    spot = slot * inner + place
+    side = place // cores
+    core = lax.rem(place, cores)
+    slot = lax.rem(group, 2)
+    mirror = group + 1 - 2 * slot
+    token_count, width = tokens_grad.shape
 
     def loop(start, stop, body):
         def wrapped(step, carry):
@@ -138,18 +156,36 @@
 
         lax.fori_loop(start, stop, wrapped, 0)
 
-    def column_range(s):
-        return pl.ds(pl.multiple_of(s * columns, LANES), columns)
-
+    def flip(r):
+        there = line
+        for bit in bits:
+            if r & bit:
+                there = there + bit * (1 - 2 * lax.rem(there // bit, 2))
+        return there
+
+    def at_line(r, s, c):
+        return flip(r) * inner + s * cores + c
+
+    def to_member(source, target, send, recv, p):
+        return pltpu.make_async_remote_copy(
+            src_ref=source,
+            dst_ref=target,
+            send_sem=send,
+            recv_sem=recv,
+            device_id={"mem": p},
+            device_id_type=MESH,
+        )
+
+    half = pl.ds(pl.multiple_of(slot * columns, LANES), columns)
     loads = [
         pltpu.make_async_copy(source, target, load_sem.at[index])
         for index, (source, target) in enumerate(
             (
-                (coarse_hbm, coarse_w),
+                (tokens_hbm, both.at[0]),
+                (cotangent_hbm, both.at[1]),
+                (coarse_hbm.at[:, :, half], coarse_w.at[:, line, side, core]),
                 (fine_hbm, fine_w),
                 (middle_hbm, middle_w),
-                (tokens_hbm, tokens),
-                (cotangent_hbm, cotangent),
             )
         )
     ]
@@ -166,56 +202,95 @@
         pl.semaphore_signal(barrier, inc=1, device_id=where, device_id_type=MESH)
 
     loop(1, count, greet)
-    own_columns = coarse_w.at[:, :, column_range(slot)]
-    loads[0].wait()
-    line_self = pltpu.make_async_copy(own_columns, coarse_line.at[line], local_sem.at[0])
-    line_self.start()
+    for load in loads[:3]:
+        load.wait()
     pl.semaphore_wait(barrier, count - 1)
 
-    def path_copy(step, landing_own):
-        other, where = anyone(step)
+    def path_copy(step):
+        _, where = anyone(step)
         return pltpu.make_async_remote_copy(
             src_ref=path_row,
-            dst_ref=all_paths.at[device if landing_own else other],
-            send_sem=path_send.at[other],
-            recv_sem=path_recv.at[device if landing_own else other],
+            dst_ref=all_paths.at[device],
+            send_sem=path_send,
+            recv_sem=path_recv,
             device_id=where,
             device_id_type=MESH,
         )
 
-    loop(1, count, lambda step: path_copy(step, True).start())
+    loop(1, count, lambda step: path_copy(step).start())
     all_paths[device] = path_row[...]
 
-    def line_copy(index, source, target, step, landing_own):
-        other = lax.rem(line + step, outer)
-        landing = line if landing_own else other
+    def pair_copy(index, source, target):
         return pltpu.make_async_remote_copy(
-            src_ref=source(other),
-            dst_ref=target.at[landing],
-            send_sem=line_send.at[index, other],
-            recv_sem=line_recv.at[index, landing],
-            device_id={"mem": other * inner + place},
+            src_ref=source,
+            dst_ref=target,
+            send_sem=pair_send.at[index],
+            recv_sem=pair_recv.at[index],
+            device_id={"grp": mirror},
             device_id_type=MESH,
         )
 
-    first_stage = (0, lambda other: own_columns, coarse_line)
-    loop(1, outer, lambda step: line_copy(*first_stage, step, True).start())
-
-    for load in loads[1:]:
+    def gather_copy(r, bit):
+        piece = coarse_w.at[:, flip(r), side, core]
+        return to_member(
+            piece,
+            piece,
+            gather_send.at[r, bits.index(bit)],
+            gather_recv.at[r ^ bit],
+            at_line(bit, side, core),
+        )
+
+    def gather_wait(r):
+        piece = coarse_w.at[:, flip(r), side, core]
+        bit = r & -r
+        to_member(
+            piece, piece, gather_send.at[0, 0], gather_recv.at[r], at_line(bit, side, core)
+        ).wait_recv()
+
+    def gather_on(r):
+        return [bit for bit in bits if r == 0 or bit < (r & -r)]
+
+    def side_copy(r, step, landing_own):
+        there = lax.rem(side + step, sides)
+        landing = side if landing_own else lax.rem(side + sides - step, sides)
+        piece = coarse_w.at[:, flip(r), landing, core]
+        return to_member(
+            piece, piece, side_send.at[0, r, step], side_recv.at[0, r, step], at_line(0, there, core)
+        )
+
+    def core_copy(r, landing_own):
+        piece = coarse_w.at[:, flip(r), :, core if landing_own else 1 - core]
+        return to_member(
+            piece, piece, core_send.at[0, r], core_recv.at[0, r], at_line(0, side, 1 - core)
+        )
+
+    tokens_pair = pair_copy(0, both.at[1 - slot], other_doc)
+
+    def pass_on(r):
+        for bit in gather_on(r):
+            gather_copy(r, bit).start()
+        for step in range(1, sides):
+            side_copy(r, step, True).start()
+
+    def share(r):
+        for step in range(1, sides):
+            side_copy(r, step, False).wait_recv()
+        if cores > 1:
+            core_copy(r, True).start()
+
+    pass_on(0)
+    tokens_pair.start()
+    for which in range(2):
+        for start in range(0, width, LANES):
+            part = slice(start, start + LANES)
+            flipped[which, part, :] = both[which, :, part].T
+    for load in loads[3:]:
         load.wait()
-    width = tokens.shape[1]
-    for start in range(0, width, LANES):
-        part = slice(start, start + LANES)
-        xt[part, :] = tokens[:, part].T
-        gt[part, :] = cotangent[:, part].T
-
-    def path_done(step):
-        done = path_copy(step, False)
-        done.wait_recv()
-        done.wait_send()
-
-    loop(1, count, path_done)
-    scalars = pltpu.make_async_copy(all_paths, path, local_sem.at[1])
+    pair_t[:, :token_count] = flipped[slot]
+
+    others = all_paths.at[pl.ds(0, count - 1)]
+    pltpu.make_async_copy(others, others, path_recv).wait()
+    scalars = pltpu.make_async_copy(all_paths, path, local_sem.at[0])
     scalars.start()
     scalars.wait()
 
@@ -224,13 +299,12 @@
 
     def member_copy(index, source, target, p, landing_own):
         landing = me if landing_own else p
-        return pltpu.make_async_remote_copy(
-            src_ref=source.at[p],
-            dst_ref=target.at[landing],
-            send_sem=mem_send.at[index, p],
-            recv_sem=mem_recv.at[index, landing],
-            device_id={"mem": p},
-            device_id_type=MESH,
+        return to_member(
+            source.at[p],
+            target.at[landing],
+            mem_send.at[index, p],
+            mem_recv.at[index, landing],
+            p,
         )
 
     def spread(index, source, target):
@@ -281,21 +355,6 @@
     def group_left(*what):
         loop(1, groups, lambda step: group_copy(*what, step, False).wait_send())
 
-    def team_copy(index, source, target, step, landing_own):
-        other = lax.rem(spot + step, size)
-        landing = spot if landing_own else other
-        return pltpu.make_async_remote_copy(
-            src_ref=source(other),
-            dst_ref=target(landing),
-            send_sem=team_send.at[index, other],
-            recv_sem=team_recv.at[index, landing],
-            device_id=(team_first + other // inner, line * inner + lax.rem(other, inner)),
-            device_id_type=MESH,
-        )
-
-    def team_document(t):
-        return (team_first + t // inner) * members + line * inner + lax.rem(t, inner)
-
     def pick_fine(index):
         held = jnp.clip(route(index, 2) - group * owned, 0, owned - 1)
         fine_out[index // members, lax.rem(index, members)] = fine_w[held]
@@ -311,6 +370,18 @@
     fine_in[group] = fine_out[group]
     middle_block[me] = middle_send[me]
 
+    share(0)
+    for r in (r for r in range(1, outer) if r % 2):
+        if r == 1:
+            gather_wait(r)
+            pass_on(r)
+    for r in range(2, outer, 2):
+        gather_wait(r)
+        pass_on(r)
+    tokens_pair.wait_recv()
+    for start in range(0, width, LANES):
+        pair_t[start : start + LANES, token_count:] = other_doc[:, start : start + LANES].T
+
     def merge_fine(p):
         owner = route(group * members + p, 2) // owned
         fine_send[p] = fine_in[owner, p]
@@ -320,33 +391,34 @@
     spread(1, fine_send, fine_block)
     fine_block[me] = fine_send[me]
 
-    line_self.wait()
-    loop(1, outer, lambda step: line_copy(*first_stage, step, False).wait_recv())
-
-    def pick_coarse(t):
-        identity = route(team_document(t), 0)
-        for z in range(outer):
-            coarse_send[t, z] = coarse_line[z, identity]
-
-    loop(0, size, pick_coarse)
-
-    def piece_of(ref, t, s):
-        return ref.at[:, lax.rem(t, inner), :, column_range(s)]
-
-    second_stage = (
-        0,
-        lambda other: coarse_send.at[other],
-        lambda landing: piece_of(coarse_block, landing, landing // inner),
-    )
-    loop(1, size, lambda step: team_copy(*second_stage, step, True).start())
-    block_self = pltpu.make_async_copy(
-        coarse_send.at[spot], piece_of(coarse_block, place, slot), local_sem.at[2]
-    )
-    block_self.start()
+    if outer > 1:
+        share(1)
+    for r in range(2, outer, 2):
+        share(r)
+    for r in range(3, outer, 2):
+        gather_wait(r)
+        pass_on(r)
+    for r in range(3, outer, 2):
+        share(r)
+    if cores > 1:
+        for r in range(outer):
+            core_copy(r, False).wait_recv()
+
+    own_block = route(device, 0)
+    other_block = route(mirror * members + me, 0)
+
+    def coarse_of(k):
+        return coarse_w[k].reshape(width, columns)
+
+    first = slot == 0
+    pre_give[...] = dot(other_doc[...], coarse_of(other_block))
+    pre_pair = pair_copy(1, pre_give, pre_take)
+    pre_pair.start()
+    pre_own = dot(both[slot], coarse_of(own_block))
 
     def compute(block, term):
         weights = block[...].reshape(width, block.shape[-1])
-        value, part = level(weights, tokens[...], cotangent[...], xt[...], gt[...])
+        value, part = level(weights, both[0], both[1], flipped[0], flipped[1])
         term[...] = value.reshape(term.shape)
         return part
 
@@ -358,25 +430,97 @@
     spread(2, middle_term, middle_own)
     middle_parts[group, me] = middle_term[me]
 
-    loop(1, size, lambda step: team_copy(*second_stage, step, False).wait_recv())
-    block_self.wait()
-    total[...] += compute(coarse_block, coarse_term)
-    gather_terms = (
-        1,
-        lambda other: piece_of(coarse_term, other, other // inner),
-        lambda landing: coarse_terms_in.at[landing],
+    pre_pair.wait_recv()
+    pre_other = pre_take[...]
+    hidden, before_grad = gelu_parts(
+        jnp.where(first, pre_own, pre_other), jnp.where(first, pre_other, pre_own)
     )
-    loop(1, size, lambda step: team_copy(*gather_terms, step, True).start())
-    term_self = pltpu.make_async_copy(
-        piece_of(coarse_term, place, slot), coarse_terms_in.at[spot], local_sem.at[3]
-    )
-    term_self.start()
+    hidden, before_grad = hidden.astype(F32), before_grad.astype(F32)
+    act_give[...] = jnp.where(first, hidden, before_grad).astype(BF16)
+    act_own = jnp.where(first, before_grad, hidden).astype(BF16)
+    act_pair = pair_copy(2, act_give, act_take)
+    act_pair.start()
+
+    @pl.when(first)
+    def _():
+        total[...] += dot_transposed(act_own, coarse_of(own_block))
+
+    act_pair.wait_recv()
+    act_other = act_take[...]
+    back = pair_copy(3, back_give, back_take)
+
+    for k in range(blocks):
+        mine = jnp.where(own_block == k, act_own.astype(F32), 0.0).astype(BF16)
+        theirs = jnp.where(other_block == k, act_other.astype(F32), 0.0).astype(BF16)
+        value = dot(pair_t[...], jnp.concatenate([mine, theirs], axis=0))
+        sums[:, :, :, k] = value.astype(BF16).reshape(outer, sides, cores, rows, columns)
+
+    order = [r for r in range(outer - 1, -1, -1)]
+
+    def fold_core(r):
+        return to_member(
+            sums.at[flip(r), :, 1 - core],
+            from_core.at[r],
+            core_send.at[1, r],
+            core_recv.at[1, r],
+            at_line(0, side, 1 - core),
+        )
+
+    def fold_side(r, step):
+        there = lax.rem(side + step, sides)
+        return to_member(
+            sums.at[flip(r), there, core],
+            from_side.at[r, step],
+            side_send.at[1, r, step],
+            side_recv.at[1, r, step],
+            at_line(0, there, core),
+        )
+
+    def fold_line(r, bit):
+        return to_member(
+            sums.at[flip(r), side, core],
+            from_line.at[r ^ bit, bits.index(bit)],
+            fold_send.at[r],
+            fold_recv.at[r ^ bit, bits.index(bit)],
+            at_line(bit, side, core),
+        )
+
+    def fold_line_wait(r, bit):
+        to_member(
+            sums.at[flip(r), side, core],
+            from_line.at[r, bits.index(bit)],
+            fold_send.at[r],
+            fold_recv.at[r, bits.index(bit)],
+            at_line(bit, side, core),
+        ).wait_recv()
+
+    def lower(r):
+        return [bit for bit in reversed(bits) if r == 0 or bit < (r & -r)]
+
+    if cores > 1:
+        for r in order:
+            fold_core(r).start()
+
+    @pl.when(first)
+    def _():
+        back_give[...] = dot_transposed(act_other, coarse_of(other_block)).astype(BF16)
+        back.start()
+
+    for r in order:
+        if cores > 1:
+            fold_core(r).wait_recv()
+            for step in range(1, sides):
+                there = lax.rem(side + step, sides)
+                sums[flip(r), there, core] = (
+                    sums[flip(r), there, core].astype(F32) + from_core[r, there].astype(F32)
+                ).astype(BF16)
+        for step in range(1, sides):
+            fold_side(r, step).start()
 
     arrive(1, fine_send, fine_block)
-    part = compute(fine_block, fine_term)
+    total[...] += compute(fine_block, fine_term)
     spread(3, fine_term, fine_own)
     fine_parts[group, me] = fine_term[me]
-    tokens_grad[...] = (total[...] + part).astype(BF16)
 
     def hand_on(target, send_on, recv_on, p, step, landing_own):
         other = lax.rem(group + step, groups)
@@ -417,49 +561,61 @@
 
     relay(2, middle_term, middle_parts, middle_send_on, middle_recv_on)
 
-    loop(1, size, lambda step: team_copy(*gather_terms, step, False).wait_recv())
-    term_self.wait()
-    step_rows = min(rows, 16)
-    weight = [
-        [jnp.where(route(team_document(t), 0) == k, 1.0, 0.0) for k in range(coarse_count)]
-        for t in range(size)
-    ]
-
-    def add_terms(index):
-        z = index // (rows // step_rows)
-        some = pl.ds(pl.multiple_of(lax.rem(index, rows // step_rows) * step_rows, step_rows), step_rows)
-        pieces = [coarse_terms_in[t, z, some, :].astype(F32) for t in range(size)]
-        for k in range(coarse_count):
-            value = pieces[0] * weight[0][k]
-            for t in range(1, size):
-                value = value + pieces[t] * weight[t][k]
-            coarse_sums[z, k, some, :] = value.astype(BF16)
-
-    loop(0, outer * (rows // step_rows), add_terms)
-    sum_stage = (1, lambda other: coarse_sums.at[other], coarse_sums_in)
-    loop(1, outer, lambda step: line_copy(*sum_stage, step, True).start())
-    coarse_sums_in[line] = coarse_sums[line]
+    def folded(r):
+        value = sums[flip(r), side, core].astype(F32)
+        if cores > 1:
+            value = value + from_core[r, side].astype(F32)
+        for step in range(1, sides):
+            value = value + from_side[r, step].astype(F32)
+        for bit in lower(r):
+            value = value + from_line[r, bits.index(bit)].astype(F32)
+        return value
+
+    for r in order:
+        for step in range(1, sides):
+            fold_side(r, step).wait_recv()
+        for bit in lower(r):
+            fold_line_wait(r, bit)
+        if r:
+            sums[flip(r), side, core] = folded(r).astype(BF16)
+            fold_line(r, r & -r).start()
+        else:
+            coarse_total[...] = folded(0).astype(BF16)
+
+    coarse_trade = (1, lambda other: coarse_total, coarse_parts)
+    group_spread(*coarse_trade)
+    coarse_parts[group] = coarse_total[...]
     relay(3, fine_term, fine_parts, fine_send_on, fine_recv_on)
 
-
+    @pl.when(first)
+    def _():
+        tokens_grad[...] = total[...].astype(BF16)
+        back.wait_send()
+
+    @pl.when(slot == 1)
+    def _():
+        back.wait_recv()
+        tokens_grad[...] = (total[...] + back_take[...].astype(F32)).astype(BF16)
+
+    pltpu.make_async_copy(others, others, path_send).wait()
+    for copy in (tokens_pair, pre_pair, act_pair):
+        copy.wait_send()
+    for r in range(outer):
+        for bit in gather_on(r):
+            gather_copy(r, bit).wait_send()
+        for step in range(1, sides):
+            side_copy(r, step, True).wait_send()
+            fold_side(r, step).wait_send()
+        if cores > 1:
+            core_copy(r, True).wait_send()
+            fold_core(r).wait_send()
+        if r:
+            fold_line(r, r & -r).wait_send()
     left(0, middle_send, middle_block)
     left(1, fine_send, fine_block)
     group_left(*fine_trade)
-    loop(1, outer, lambda step: line_copy(*first_stage, step, False).wait_send())
-    loop(1, size, lambda step: team_copy(*second_stage, step, False).wait_send())
-    loop(1, size, lambda step: team_copy(*gather_terms, step, False).wait_send())
     left(2, middle_term, middle_own)
     left(3, fine_term, fine_own)
-
-    loop(1, outer, lambda step: line_copy(*sum_stage, step, False).wait_recv())
-    value = coarse_sums_in[0].astype(F32)
-    for z in range(1, outer):
-        value = value + coarse_sums_in[z].astype(F32)
-    coarse_total[...] = value.astype(BF16)
-    coarse_trade = (1, lambda other: coarse_total, coarse_parts)
-    group_spread(*coarse_trade)
-    coarse_parts[group] = coarse_total[...]
-    loop(1, outer, lambda step: line_copy(*sum_stage, step, False).wait_send())
     group_arrive(*coarse_trade)
     group_left(*coarse_trade)
     relay_done(middle_parts, middle_send_on, middle_recv_on)
@@ -471,9 +627,9 @@
     medium, narrow = middle_w.shape[2], fine_w.shape[2]
     token_count, width = tokens.shape
     count = groups * members
-    outer, inner, team = plan(groups, members, wide)
-    columns = wide // team
-    size = team * inner
+    outer, sides, cores = plan(groups, members, wide)
+    steps = max(len(bits_of(outer)), 1)
+    columns = wide // 2
 
     def stack(*shape):
         return pltpu.VMEM(shape, BF16)
@@ -495,41 +651,50 @@
         out_specs=(vmem,) * 5,
         scratch_shapes=[
             pltpu.SMEM((count,) + path.shape, jnp.int32),
+            stack(2, *tokens.shape),
             stack(*tokens.shape),
-            stack(*cotangent.shape),
-            stack(*coarse_w.shape),
+            stack(blocks, outer, sides, cores, rows, columns),
             stack(*middle_w.shape),
             stack(*fine_w.shape),
             stack(members, rows, medium),
             stack(groups, members, rows, narrow),
             stack(groups, members, rows, narrow),
             stack(members, rows, narrow),
-            stack(outer, blocks, rows, columns),
-            stack(size, outer, rows, columns),
-            stack(outer, inner, rows, wide),
             stack(members, rows, medium),
             stack(members, rows, narrow),
-            stack(outer, inner, rows, wide),
             stack(members, rows, medium),
             stack(members, rows, narrow),
-            stack(size, outer, rows, columns),
-            stack(outer, blocks, rows, columns),
-            stack(outer, blocks, rows, columns),
+            stack(outer, sides, cores, blocks, rows, columns),
+            stack(outer, sides, blocks, rows, columns),
+            stack(outer, sides, blocks, rows, columns),
+            stack(outer, steps, blocks, rows, columns),
             stack(blocks, rows, columns),
-            stack(width, token_count),
-            stack(width, token_count),
+            stack(2, width, token_count),
+            stack(width, 2 * token_count),
             pltpu.VMEM((token_count, width), F32),
-            sems(count),
-            sems(count),
+            pltpu.VMEM((token_count, columns), F32),
+            pltpu.VMEM((token_count, columns), F32),
+            stack(token_count, columns),
+            stack(token_count, columns),
+            stack(token_count, width),
+            stack(token_count, width),
+            pltpu.SemaphoreType.DMA,
+            pltpu.SemaphoreType.DMA,
             sems(4, members),
             sems(4, members),
             sems(2, groups),
             sems(2, groups),
+            sems(4),
+            sems(4),
+            sems(outer, steps),
+            sems(outer),
+            sems(2, outer, sides),
+            sems(2, outer, sides),
             sems(2, outer),
             sems(2, outer),
-            sems(2, size),
-            sems(2, size),
-            sems(4),
+            sems(outer),
+            sems(outer, steps),
+            sems(1),
             sems(5),
             sems(groups, members),
             sems(groups, members),

time: 87.8 us -> 83.9 us (0.956)
  the two profiles are of different devices: /device:TPU:11 before, /device:TPU:0 now
where the time goes in v1:
time: 83.9 us; the launch traced here: 83.6 us
  Pallas kernels  83 us (99%)
    pallas_call x1, Pallas kernels, exchange(): pl.pallas_call(functools.partial(main_kernel, groups, members), out_shape...  78.1 us
    pallas_call x1, Pallas kernels, collect(): pl.pallas_call(collect_kernel, out_shape=tuple((jax.ShapeDtypeStruct(shap...  4.88 us

profile of v1, /device:TPU:0, one launch (start us, length us, event | category | flops | bytes accessed | tf_op | source)
XLA Modules:
  0.0 83.6 jit_solution(7603175166218456204)
XLA Ops:
  0.6 78.1 %exchange.1 = (s32[32,1,3]{2,1,0:T(1,128)}, bf16[128,1024]{1,0:T(8,128)(2,1)}, bf16[2,16,64,256]{3,2,1,0:T(8,128)(2,1)}, bf16[2,16,64,128]{3,2,1,0:T(8,128)(2,1)}, bf16[2,4,64,256]{3,2,1,0:T(8,128)(2,1)}) custom-call(s32[1,3]{1,0:T(1,128)} %path_row.1, bf16[128,1024]{1,0:T(8,128)(2,1)} %tokens_hbm.1, bf16[128,1024]{1,0:T(8,128)(2,1)} %cotangent_hbm.1, ...), custom_call_target="tpu_custom_call" | custom-call | tf_op jit(solution)/shard_map/exchange/pallas_call | solution.py:641
  78.7 4.9 %collect.1 = (bf16[128,1024]{1,0:T(8,128)(2,1)}, bf16[4,64,512]{2,1,0:T(8,128)(2,1)}, bf16[64,64,256]{2,1,0:T(8,128)(2,1)}, bf16[32,64,128]{2,1,0:T(8,128)(2,1)}) custom-call(s32[32,1,3]{2,1,0:T(1,128)} %get-tuple-element.9.path, s32[1]{0:T(128)} %bitcast.first_owned, bf16[128,1024]{1,0:T(8,128)(2,1)} %get-tuple-element.10.tokens_in, ...), custom_call_target="tpu_custom_call" | custom-call | tf_op jit(solution)/shard_map/collect/pallas_call | solution.py:786

commit v2 on v1

--- a/solution.py
+++ b/solution.py
@@ -77,6 +77,11 @@
     coarse_hbm,
     middle_hbm,
     fine_hbm,
+    paths_out,
+    tokens_out,
+    middle_out,
+    fine_parts_out,
+    coarse_out,
     all_paths,
     tokens_grad,
     middle_parts,
@@ -114,6 +119,7 @@
     path_recv,
     mem_send,
     mem_recv,
+    weight_recv,
     grp_send,
     grp_recv,
     pair_send,
@@ -128,6 +134,7 @@
     fold_recv,
     local_sem,
     load_sem,
+    out_sem,
     middle_send_on,
     middle_recv_on,
     fine_send_on,
@@ -191,6 +198,18 @@
     ]
     for load in loads:
         load.start()
+    outs = [
+        pltpu.make_async_copy(source, target, out_sem.at[index])
+        for index, (source, target) in enumerate(
+            (
+                (all_paths, paths_out),
+                (tokens_grad, tokens_out),
+                (middle_parts, middle_out),
+                (fine_parts, fine_parts_out),
+                (coarse_parts, coarse_out),
+            )
+        )
+    ]
     barrier = pltpu.get_barrier_semaphore()
 
     def anyone(step):
@@ -287,52 +306,55 @@
     for load in loads[3:]:
         load.wait()
     pair_t[:, :token_count] = flipped[slot]
+    if outer > 1:
+        gather_wait(1)
+        pass_on(1)
+    share(0)
 
     others = all_paths.at[pl.ds(0, count - 1)]
     pltpu.make_async_copy(others, others, path_recv).wait()
     scalars = pltpu.make_async_copy(all_paths, path, local_sem.at[0])
     scalars.start()
     scalars.wait()
+    outs[0].start()
 
     def route(document, column):
         return path[document, 0, column]
 
     def member_copy(index, source, target, p, landing_own):
         landing = me if landing_own else p
-        return to_member(
-            source.at[p],
-            target.at[landing],
-            mem_send.at[index, p],
-            mem_recv.at[index, landing],
-            p,
-        )
-
-    def spread(index, source, target):
+        arrived = weight_recv.at[index] if index < 2 else mem_recv.at[index - 2, landing]
+        return to_member(source.at[p], target.at[landing], mem_send.at[index], arrived, p)
+
+    def all_of(ref, number, sem):
+        some = ref.at[pl.ds(0, number)]
+        return pltpu.make_async_copy(some, some, sem)
+
+    near = outer * cores
+
+    def partner(step):
+        there = lax.rem(side + step // near, sides)
+        rest = lax.rem(step, near)
+        return (
+            lax.rem(line + rest // cores, outer) * inner
+            + there * cores
+            + lax.rem(core + lax.rem(rest, cores), cores)
+        )
+
+    def spread(index, source, target, start=1, stop=members):
         loop(
-            1,
-            members,
-            lambda step: member_copy(
-                index, source, target, lax.rem(me + step, members), True
-            ).start(),
-        )
-
-    def arrive(index, source, target):
-        loop(
-            1,
-            members,
-            lambda step: member_copy(
-                index, source, target, lax.rem(me + members - step, members), False
-            ).wait_recv(),
-        )
-
-    def left(index, source, target):
-        loop(
-            1,
-            members,
-            lambda step: member_copy(
-                index, source, target, lax.rem(me + step, members), False
-            ).wait_send(),
-        )
+            start,
+            stop,
+            lambda step: member_copy(index, source, target, partner(step), True).start(),
+        )
+
+    def arrive(index, target):
+        if members > 1:
+            all_of(target, members - 1, weight_recv.at[index]).wait()
+
+    def left(index, source):
+        if members > 1:
+            all_of(source, members - 1, mem_send.at[index]).wait()
 
     def group_copy(index, source, target, step, landing_own):
         other = lax.rem(group + step, groups)
@@ -366,21 +388,24 @@
     fine_trade = (0, lambda other: fine_out.at[other], fine_in)
     group_spread(*fine_trade)
     loop(0, members, pick_middle)
-    spread(0, middle_send, middle_block)
+    spread(0, middle_send, middle_block, 1, near)
     fine_in[group] = fine_out[group]
     middle_block[me] = middle_send[me]
 
-    share(0)
-    for r in (r for r in range(1, outer) if r % 2):
-        if r == 1:
-            gather_wait(r)
-            pass_on(r)
     for r in range(2, outer, 2):
         gather_wait(r)
         pass_on(r)
+    if outer > 1:
+        share(1)
+    for r in range(3, outer, 2):
+        gather_wait(r)
+        pass_on(r)
+    spread(0, middle_send, middle_block, near, members)
     tokens_pair.wait_recv()
     for start in range(0, width, LANES):
         pair_t[start : start + LANES, token_count:] = other_doc[:, start : start + LANES].T
+    for r in range(2, outer, 2):
+        share(r)
 
     def merge_fine(p):
         owner = route(group * members + p, 2) // owned
@@ -391,13 +416,6 @@
     spread(1, fine_send, fine_block)
     fine_block[me] = fine_send[me]
 
-    if outer > 1:
-        share(1)
-    for r in range(2, outer, 2):
-        share(r)
-    for r in range(3, outer, 2):
-        gather_wait(r)
-        pass_on(r)
     for r in range(3, outer, 2):
         share(r)
     if cores > 1:
@@ -425,7 +443,7 @@
     middle_own = middle_parts.at[group]
     fine_own = fine_parts.at[group]
 
-    arrive(0, middle_send, middle_block)
+    arrive(0, middle_block)
     total[...] = compute(middle_block, middle_term)
     spread(2, middle_term, middle_own)
     middle_parts[group, me] = middle_term[me]
@@ -455,7 +473,7 @@
         value = dot(pair_t[...], jnp.concatenate([mine, theirs], axis=0))
         sums[:, :, :, k] = value.astype(BF16).reshape(outer, sides, cores, rows, columns)
 
-    order = [r for r in range(outer - 1, -1, -1)]
+    order = list(range(outer - 1, 0, -2)) + list(range(outer - 2, 0, -2)) + [0]
 
     def fold_core(r):
         return to_member(
@@ -517,7 +535,7 @@
         for step in range(1, sides):
             fold_side(r, step).start()
 
-    arrive(1, fine_send, fine_block)
+    arrive(1, fine_block)
     total[...] += compute(fine_block, fine_term)
     spread(3, fine_term, fine_own)
     fine_parts[group, me] = fine_term[me]
@@ -528,8 +546,8 @@
         return pltpu.make_async_remote_copy(
             src_ref=target.at[group, p],
             dst_ref=target.at[landing, p],
-            send_sem=send_on.at[other, p],
-            recv_sem=recv_on.at[landing, p],
+            send_sem=send_on,
+            recv_sem=recv_on,
             device_id={"grp": other},
             device_id_type=MESH,
         )
@@ -549,15 +567,9 @@
         loop(1, members, body)
 
     def relay_done(target, send_on, recv_on):
-        def body(index):
-            p = index // (groups - 1)
-            step = lax.rem(index, groups - 1) + 1
-            done = hand_on(target, send_on, recv_on, p, step, False)
-            done.wait_recv()
-            done.wait_send()
-
         if groups > 1:
-            loop(0, members * (groups - 1), body)
+            all_of(target, groups - 1, recv_on).wait()
+            all_of(target, groups - 1, send_on).wait()
 
     relay(2, middle_term, middle_parts, middle_send_on, middle_recv_on)
 
@@ -579,13 +591,14 @@
         if r:
             sums[flip(r), side, core] = folded(r).astype(BF16)
             fold_line(r, r & -r).start()
+            if r == order[-2]:
+                relay(3, fine_term, fine_parts, fine_send_on, fine_recv_on)
         else:
             coarse_total[...] = folded(0).astype(BF16)
 
     coarse_trade = (1, lambda other: coarse_total, coarse_parts)
     group_spread(*coarse_trade)
     coarse_parts[group] = coarse_total[...]
-    relay(3, fine_term, fine_parts, fine_send_on, fine_recv_on)
 
     @pl.when(first)
     def _():
@@ -597,6 +610,7 @@
         back.wait_recv()
         tokens_grad[...] = (total[...] + back_take[...].astype(F32)).astype(BF16)
 
+    outs[1].start()
     pltpu.make_async_copy(others, others, path_send).wait()
     for copy in (tokens_pair, pre_pair, act_pair):
         copy.wait_send()
@@ -611,15 +625,20 @@
             fold_core(r).wait_send()
         if r:
             fold_line(r, r & -r).wait_send()
-    left(0, middle_send, middle_block)
-    left(1, fine_send, fine_block)
+    left(0, middle_send)
+    left(1, fine_send)
     group_left(*fine_trade)
-    left(2, middle_term, middle_own)
-    left(3, fine_term, fine_own)
+    left(2, middle_term)
+    left(3, fine_term)
+    relay_done(middle_parts, middle_send_on, middle_recv_on)
+    outs[2].start()
+    relay_done(fine_parts, fine_send_on, fine_recv_on)
+    outs[3].start()
     group_arrive(*coarse_trade)
+    outs[4].start()
     group_left(*coarse_trade)
-    relay_done(middle_parts, middle_send_on, middle_recv_on)
-    relay_done(fine_parts, fine_send_on, fine_recv_on)
+    for out in outs:
+        out.wait()
 
 
 def exchange(path, tokens, cotangent, coarse_w, middle_w, fine_w, groups, members):
@@ -648,8 +667,13 @@
             jax.ShapeDtypeStruct((groups, blocks, rows, columns), BF16),
         ),
         in_specs=[vmem] + [pl.BlockSpec(memory_space=pl.ANY)] * 5,
-        out_specs=(vmem,) * 5,
+        out_specs=(pl.BlockSpec(memory_space=pl.ANY),) * 5,
         scratch_shapes=[
+            pltpu.VMEM((count,) + path.shape, jnp.int32),
+            stack(*tokens.shape),
+            stack(groups, members, rows, medium),
+            stack(groups, members, rows, narrow),
+            stack(groups, blocks, rows, columns),
             pltpu.SMEM((count,) + path.shape, jnp.int32),
             stack(2, *tokens.shape),
             stack(*tokens.shape),
@@ -680,8 +704,9 @@
             stack(token_count, width),
             pltpu.SemaphoreType.DMA,
             pltpu.SemaphoreType.DMA,
-            sems(4, members),
-            sems(4, members),
+            sems(4),
+            sems(2, members),
+            sems(2),
             sems(2, groups),
             sems(2, groups),
             sems(4),
@@ -696,10 +721,11 @@
             sems(outer, steps),
             sems(1),
             sems(5),
-            sems(groups, members),
-            sems(groups, members),
-            sems(groups, members),
-            sems(groups, members),
+            sems(5),
+            pltpu.SemaphoreType.DMA,
+            pltpu.SemaphoreType.DMA,
+            pltpu.SemaphoreType.DMA,
+            pltpu.SemaphoreType.DMA,
         ],
         compiler_params=pltpu.CompilerParams(
             collective_id=0, has_side_effects=True, vmem_limit_bytes=60 * 2**20

time: 83.9 us -> 77.3 us (0.921)
  Pallas kernels: 83 us -> 75.6 us
    pallas_call x1, Pallas kernels: 78.1 us -> 70.7 us  [exchange(): pl.pallas_call(functools.partial(main_kernel, groups, members), out_shape...]
where the time goes in v2:
time: 77.3 us; the launch traced here: 76.3 us
  Pallas kernels  75.6 us (98%)
    pallas_call x1, Pallas kernels, exchange(): pl.pallas_call(functools.partial(main_kernel, groups, members), out_shape...  70.7 us
    pallas_call x1, Pallas kernels, collect(): pl.pallas_call(collect_kernel, out_shape=tuple((jax.ShapeDtypeStruct(shap...  4.88 us

profile of v2, /device:TPU:0, one launch (start us, length us, event | category | flops | bytes accessed | tf_op | source)
XLA Modules:
  0.0 76.3 jit_solution(3976963142312565683)
XLA Ops:
  0.6 70.7 %exchange.1 = (s32[32,1,3]{2,1,0:T(1,128)}, bf16[128,1024]{1,0:T(8,128)(2,1)}, bf16[2,16,64,256]{3,2,1,0:T(8,128)(2,1)}, bf16[2,16,64,128]{3,2,1,0:T(8,128)(2,1)}, bf16[2,4,64,256]{3,2,1,0:T(8,128)(2,1)}) custom-call(s32[1,3]{1,0:T(1,128)} %path_row.1, bf16[128,1024]{1,0:T(8,128)(2,1)} %tokens_hbm.1, bf16[128,1024]{1,0:T(8,128)(2,1)} %cotangent_hbm.1, ...), custom_call_target="tpu_custom_call" | custom-call | tf_op jit(solution)/shard_map/exchange/pallas_call | solution.py:660
  71.4 4.9 %collect.1 = (bf16[128,1024]{1,0:T(8,128)(2,1)}, bf16[4,64,512]{2,1,0:T(8,128)(2,1)}, bf16[64,64,256]{2,1,0:T(8,128)(2,1)}, bf16[32,64,128]{2,1,0:T(8,128)(2,1)}) custom-call(s32[32,1,3]{2,1,0:T(1,128)} %get-tuple-element.9.path, s32[1]{0:T(128)} %bitcast.first_owned, bf16[128,1024]{1,0:T(8,128)(2,1)} %get-tuple-element.10.tokens_in, ...), custom_call_target="tpu_custom_call" | custom-call | tf_op jit(solution)/shard_map/collect/pallas_call | solution.py:812

commit v3 on v2

--- a/solution.py
+++ b/solution.py
@@ -54,9 +54,11 @@
     return term, dot_transposed(grad, weights)
 
 
-def plan(groups, members, blocks_width):
+def plan(members, rows):
     inner = max(k for k in range(1, math.isqrt(members) + 1) if members % k == 0)
-    cores = 2 if inner % 2 == 0 else 1
+    cores = next(
+        k for k in range(1, inner + 1) if inner % k == 0 and (k * rows % LANES == 0 or k == inner)
+    )
     return members // inner, inner // cores, cores
 
 
@@ -89,7 +91,7 @@
     coarse_parts,
     path,
     both,
-    other_doc,
+    docs,
     coarse_w,
     middle_w,
     fine_w,
@@ -103,14 +105,14 @@
     fine_term,
     sums,
     from_core,
-    from_side,
     from_line,
     coarse_total,
     flipped,
-    pair_t,
+    quad_t,
     total,
     pre_give,
     pre_take,
+    act_keep,
     act_give,
     act_take,
     back_give,
@@ -122,18 +124,17 @@
     weight_recv,
     grp_send,
     grp_recv,
-    pair_send,
-    pair_recv,
+    quad_send,
+    quad_recv,
     gather_send,
     gather_recv,
-    side_send,
-    side_recv,
     core_send,
     core_recv,
     fold_send,
     fold_recv,
     local_sem,
     load_sem,
+    token_sem,
     out_sem,
     middle_send_on,
     middle_recv_on,
@@ -145,8 +146,10 @@
     count = groups * members
     device = group * members + me
     owned = fine_w.shape[0]
-    blocks, outer, sides, cores, rows, columns = coarse_w.shape
+    blocks, outer, cores, rows, columns = coarse_w.shape
+    _, _, sides, token_count, span = both.shape
     inner = sides * cores
+    depth = outer * span
     bits = bits_of(outer)
     line = me // inner
     place = lax.rem(me, inner)
@@ -154,7 +157,7 @@
     core = lax.rem(place, cores)
     slot = lax.rem(group, 2)
     mirror = group + 1 - 2 * slot
-    token_count, width = tokens_grad.shape
+    width = tokens_grad.shape[1]
 
     def loop(start, stop, body):
         def wrapped(step, carry):
@@ -188,15 +191,26 @@
         pltpu.make_async_copy(source, target, load_sem.at[index])
         for index, (source, target) in enumerate(
             (
-                (tokens_hbm, both.at[0]),
-                (cotangent_hbm, both.at[1]),
-                (coarse_hbm.at[:, :, half], coarse_w.at[:, line, side, core]),
+                (coarse_hbm.at[:, :, half], coarse_w.at[:, line, core]),
                 (fine_hbm, fine_w),
                 (middle_hbm, middle_w),
             )
         )
     ]
-    for load in loads:
+    places = [(o, a) for o in range(outer) for a in range(sides)]
+    token_loads = [
+        pltpu.make_async_copy(
+            source.at[:, pl.ds(index * span, span)],
+            both.at[which, o, a],
+            token_sem.at[which, index],
+        )
+        for which, source in enumerate((tokens_hbm, cotangent_hbm))
+        for index, (o, a) in enumerate(places)
+    ]
+    loads[0].start()
+    for load in token_loads:
+        load.start()
+    for load in loads[1:]:
         load.start()
     outs = [
         pltpu.make_async_copy(source, target, out_sem.at[index])
@@ -221,8 +235,7 @@
         pl.semaphore_signal(barrier, inc=1, device_id=where, device_id_type=MESH)
 
     loop(1, count, greet)
-    for load in loads[:3]:
-        load.wait()
+    loads[0].wait()
     pl.semaphore_wait(barrier, count - 1)
 
     def path_copy(step):
@@ -239,18 +252,28 @@
     loop(1, count, lambda step: path_copy(step).start())
     all_paths[device] = path_row[...]
 
-    def pair_copy(index, source, target):
+    quad = [(dy, da) for dy in range(2) for da in range(sides)]
+    peers = quad[1:]
+
+    def quad_side(da):
+        return lax.rem(side + da, sides)
+
+    def quad_copy(stage, source, target, dy, da):
+        back_da = (sides - da) % sides
         return pltpu.make_async_remote_copy(
             src_ref=source,
-            dst_ref=target,
-            send_sem=pair_send.at[index],
-            recv_sem=pair_recv.at[index],
-            device_id={"grp": mirror},
+            dst_ref=target.at[dy, back_da],
+            send_sem=quad_send.at[stage, dy, da],
+            recv_sem=quad_recv.at[stage, dy, back_da],
+            device_id=(mirror if dy else group, at_line(0, quad_side(da), core)),
             device_id_type=MESH,
         )
 
+    def quad_wait(stage, source, target, dy, da):
+        quad_copy(stage, source, target, dy, (sides - da) % sides).wait_recv()
+
     def gather_copy(r, bit):
-        piece = coarse_w.at[:, flip(r), side, core]
+        piece = coarse_w.at[:, flip(r), core]
         return to_member(
             piece,
             piece,
@@ -260,7 +283,7 @@
         )
 
     def gather_wait(r):
-        piece = coarse_w.at[:, flip(r), side, core]
+        piece = coarse_w.at[:, flip(r), core]
         bit = r & -r
         to_member(
             piece, piece, gather_send.at[0, 0], gather_recv.at[r], at_line(bit, side, core)
@@ -269,48 +292,47 @@
     def gather_on(r):
         return [bit for bit in bits if r == 0 or bit < (r & -r)]
 
-    def side_copy(r, step, landing_own):
-        there = lax.rem(side + step, sides)
-        landing = side if landing_own else lax.rem(side + sides - step, sides)
-        piece = coarse_w.at[:, flip(r), landing, core]
+    def core_copy(r, step, landing_own):
+        there = lax.rem(core + step, cores)
+        landing = core if landing_own else lax.rem(core + cores - step, cores)
+        piece = coarse_w.at[:, flip(r), landing]
         return to_member(
-            piece, piece, side_send.at[0, r, step], side_recv.at[0, r, step], at_line(0, there, core)
-        )
-
-    def core_copy(r, landing_own):
-        piece = coarse_w.at[:, flip(r), :, core if landing_own else 1 - core]
-        return to_member(
-            piece, piece, core_send.at[0, r], core_recv.at[0, r], at_line(0, side, 1 - core)
-        )
-
-    tokens_pair = pair_copy(0, both.at[1 - slot], other_doc)
+            piece, piece, core_send.at[0, r, step], core_recv.at[0, r, step], at_line(0, side, there)
+        )
 
     def pass_on(r):
         for bit in gather_on(r):
             gather_copy(r, bit).start()
-        for step in range(1, sides):
-            side_copy(r, step, True).start()
-
-    def share(r):
-        for step in range(1, sides):
-            side_copy(r, step, False).wait_recv()
-        if cores > 1:
-            core_copy(r, True).start()
+        for step in range(1, cores):
+            core_copy(r, step, True).start()
+
+    def doc_copy(dy, da):
+        which = 1 - slot if dy else slot
+        return quad_copy(0, both.at[which, :, quad_side(da)], docs, dy, da)
 
     pass_on(0)
-    tokens_pair.start()
+    for load in token_loads:
+        load.wait()
+    for dy, da in peers:
+        doc_copy(dy, da).start()
     for which in range(2):
-        for start in range(0, width, LANES):
-            part = slice(start, start + LANES)
-            flipped[which, part, :] = both[which, :, part].T
-    for load in loads[3:]:
+        for index, (o, a) in enumerate(places):
+            flipped[which, index * span : (index + 1) * span, :] = both[which, o, a].T
+    docs[0, 0] = both[slot, :, side]
+    for load in loads[1:]:
         load.wait()
-    pair_t[:, :token_count] = flipped[slot]
     if outer > 1:
         gather_wait(1)
         pass_on(1)
-    share(0)
-
+
+    def turn(dy, da):
+        q = dy * sides + da
+        for o in range(outer):
+            quad_t[o * span : (o + 1) * span, q * token_count : (q + 1) * token_count] = docs[
+                dy, da, o
+            ].T
+
+    turn(0, 0)
     others = all_paths.at[pl.ds(0, count - 1)]
     pltpu.make_async_copy(others, others, path_recv).wait()
     scalars = pltpu.make_async_copy(all_paths, path, local_sem.at[0])
@@ -388,24 +410,16 @@
     fine_trade = (0, lambda other: fine_out.at[other], fine_in)
     group_spread(*fine_trade)
     loop(0, members, pick_middle)
-    spread(0, middle_send, middle_block, 1, near)
+    spread(0, middle_send, middle_block)
     fine_in[group] = fine_out[group]
     middle_block[me] = middle_send[me]
 
     for r in range(2, outer, 2):
         gather_wait(r)
         pass_on(r)
-    if outer > 1:
-        share(1)
-    for r in range(3, outer, 2):
-        gather_wait(r)
-        pass_on(r)
-    spread(0, middle_send, middle_block, near, members)
-    tokens_pair.wait_recv()
-    for start in range(0, width, LANES):
-        pair_t[start : start + LANES, token_count:] = other_doc[:, start : start + LANES].T
-    for r in range(2, outer, 2):
-        share(r)
+    for dy, da in peers:
+        quad_wait(0, both.at[0, :, 0], docs, dy, da)
+        turn(dy, da)
 
     def merge_fine(p):
         owner = route(group * members + p, 2) // owned
@@ -417,86 +431,94 @@
     fine_block[me] = fine_send[me]
 
     for r in range(3, outer, 2):
-        share(r)
-    if cores > 1:
-        for r in range(outer):
-            core_copy(r, False).wait_recv()
-
-    own_block = route(device, 0)
-    other_block = route(mirror * members + me, 0)
+        gather_wait(r)
+        pass_on(r)
+    for r in range(outer):
+        for step in range(1, cores):
+            core_copy(r, step, False).wait_recv()
+
+    def block_of(dy, da):
+        who = (mirror if dy else group) * members + at_line(0, quad_side(da), core)
+        return route(who, 0)
 
     def coarse_of(k):
-        return coarse_w[k].reshape(width, columns)
+        return coarse_w[k].reshape(depth, columns)
+
+    def wide_of(dy, da):
+        return jnp.concatenate([docs[dy, da, o] for o in range(outer)], axis=1)
 
     first = slot == 0
-    pre_give[...] = dot(other_doc[...], coarse_of(other_block))
-    pre_pair = pair_copy(1, pre_give, pre_take)
-    pre_pair.start()
-    pre_own = dot(both[slot], coarse_of(own_block))
+    for dy, da in peers:
+        pre_give[dy, da] = dot(wide_of(dy, da), coarse_of(block_of(dy, da))).astype(BF16)
+        quad_copy(1, pre_give.at[dy, da], pre_take, dy, da).start()
+    pre_own = dot(wide_of(0, 0), coarse_of(block_of(0, 0)))
+    pre_other = jnp.zeros_like(pre_own)
+
+    def whole(which):
+        return jnp.concatenate([both[which, o, a] for o, a in places], axis=1)
 
     def compute(block, term):
         weights = block[...].reshape(width, block.shape[-1])
-        value, part = level(weights, both[0], both[1], flipped[0], flipped[1])
+        value, part = level(weights, whole(0), whole(1), flipped[0], flipped[1])
         term[...] = value.reshape(term.shape)
         return part
 
     middle_own = middle_parts.at[group]
     fine_own = fine_parts.at[group]
 
-    arrive(0, middle_block)
-    total[...] = compute(middle_block, middle_term)
-    spread(2, middle_term, middle_own)
-    middle_parts[group, me] = middle_term[me]
-
-    pre_pair.wait_recv()
-    pre_other = pre_take[...]
+    for dy, da in peers:
+        quad_wait(1, pre_give.at[0, 0], pre_take, dy, da)
+    for dy, da in peers:
+        if dy:
+            pre_other = pre_other + pre_take[dy, da].astype(F32)
+        else:
+            pre_own = pre_own + pre_take[dy, da].astype(F32)
     hidden, before_grad = gelu_parts(
         jnp.where(first, pre_own, pre_other), jnp.where(first, pre_other, pre_own)
     )
     hidden, before_grad = hidden.astype(F32), before_grad.astype(F32)
     act_give[...] = jnp.where(first, hidden, before_grad).astype(BF16)
-    act_own = jnp.where(first, before_grad, hidden).astype(BF16)
-    act_pair = pair_copy(2, act_give, act_take)
-    act_pair.start()
-
-    @pl.when(first)
-    def _():
-        total[...] += dot_transposed(act_own, coarse_of(own_block))
-
-    act_pair.wait_recv()
-    act_other = act_take[...]
-    back = pair_copy(3, back_give, back_take)
+    act_keep[...] = jnp.where(first, before_grad, hidden).astype(BF16)
+    act_take[0, 0] = act_keep[...]
+    for dy, da in peers:
+        quad_copy(2, act_give if dy else act_keep, act_take, dy, da).start()
+
+    arrive(0, middle_block)
+    total[...] = compute(middle_block, middle_term)
+    spread(2, middle_term, middle_own)
+    middle_parts[group, me] = middle_term[me]
+
+    arrive(1, fine_block)
+    total[...] += compute(fine_block, fine_term)
+    spread(3, fine_term, fine_own)
+    fine_parts[group, me] = fine_term[me]
+
+    for dy, da in peers:
+        quad_wait(2, act_keep, act_take, dy, da)
 
     for k in range(blocks):
-        mine = jnp.where(own_block == k, act_own.astype(F32), 0.0).astype(BF16)
-        theirs = jnp.where(other_block == k, act_other.astype(F32), 0.0).astype(BF16)
-        value = dot(pair_t[...], jnp.concatenate([mine, theirs], axis=0))
-        sums[:, :, :, k] = value.astype(BF16).reshape(outer, sides, cores, rows, columns)
+        acts = [
+            jnp.where(block_of(dy, da) == k, act_take[dy, da].astype(F32), 0.0).astype(BF16)
+            for dy, da in quad
+        ]
+        value = dot(quad_t[...], jnp.concatenate(acts, axis=0))
+        sums[:, :, k] = value.astype(BF16).reshape(outer, cores, rows, columns)
 
     order = list(range(outer - 1, 0, -2)) + list(range(outer - 2, 0, -2)) + [0]
 
-    def fold_core(r):
+    def fold_core(r, step):
+        there = lax.rem(core + step, cores)
         return to_member(
-            sums.at[flip(r), :, 1 - core],
-            from_core.at[r],
-            core_send.at[1, r],
-            core_recv.at[1, r],
-            at_line(0, side, 1 - core),
-        )
-
-    def fold_side(r, step):
-        there = lax.rem(side + step, sides)
-        return to_member(
-            sums.at[flip(r), there, core],
-            from_side.at[r, step],
-            side_send.at[1, r, step],
-            side_recv.at[1, r, step],
-            at_line(0, there, core),
+            sums.at[flip(r), there],
+            from_core.at[r, step],
+            core_send.at[1, r, step],
+            core_recv.at[1, r, step],
+            at_line(0, side, there),
         )
 
     def fold_line(r, bit):
         return to_member(
-            sums.at[flip(r), side, core],
+            sums.at[flip(r), core],
             from_line.at[r ^ bit, bits.index(bit)],
             fold_send.at[r],
             fold_recv.at[r ^ bit, bits.index(bit)],
@@ -505,7 +527,7 @@
 
     def fold_line_wait(r, bit):
         to_member(
-            sums.at[flip(r), side, core],
+            sums.at[flip(r), core],
             from_line.at[r, bits.index(bit)],
             fold_send.at[r],
             fold_recv.at[r, bits.index(bit)],
@@ -515,30 +537,20 @@
     def lower(r):
         return [bit for bit in reversed(bits) if r == 0 or bit < (r & -r)]
 
-    if cores > 1:
-        for r in order:
-            fold_core(r).start()
+    for r in order:
+        for step in range(1, cores):
+            fold_core(r, step).start()
+
+    def back_copy(dy, da):
+        return quad_copy(3, back_give.at[dy, da], back_take, dy, da)
 
     @pl.when(first)
     def _():
-        back_give[...] = dot_transposed(act_other, coarse_of(other_block)).astype(BF16)
-        back.start()
-
-    for r in order:
-        if cores > 1:
-            fold_core(r).wait_recv()
-            for step in range(1, sides):
-                there = lax.rem(side + step, sides)
-                sums[flip(r), there, core] = (
-                    sums[flip(r), there, core].astype(F32) + from_core[r, there].astype(F32)
-                ).astype(BF16)
-        for step in range(1, sides):
-            fold_side(r, step).start()
-
-    arrive(1, fine_block)
-    total[...] += compute(fine_block, fine_term)
-    spread(3, fine_term, fine_own)
-    fine_parts[group, me] = fine_term[me]
+        for dy, da in peers:
+            back_give[dy, da] = dot_transposed(
+                act_take[dy, da], coarse_of(block_of(dy, da))
+            ).astype(BF16)
+            back_copy(dy, da).start()
 
     def hand_on(target, send_on, recv_on, p, step, landing_own):
         other = lax.rem(group + step, groups)
@@ -571,27 +583,24 @@
             all_of(target, groups - 1, recv_on).wait()
             all_of(target, groups - 1, send_on).wait()
 
-    relay(2, middle_term, middle_parts, middle_send_on, middle_recv_on)
-
     def folded(r):
-        value = sums[flip(r), side, core].astype(F32)
-        if cores > 1:
-            value = value + from_core[r, side].astype(F32)
-        for step in range(1, sides):
-            value = value + from_side[r, step].astype(F32)
+        value = sums[flip(r), core].astype(F32)
+        for step in range(1, cores):
+            value = value + from_core[r, step].astype(F32)
         for bit in lower(r):
             value = value + from_line[r, bits.index(bit)].astype(F32)
         return value
 
     for r in order:
-        for step in range(1, sides):
-            fold_side(r, step).wait_recv()
+        for step in range(1, cores):
+            fold_core(r, step).wait_recv()
         for bit in lower(r):
             fold_line_wait(r, bit)
         if r:
-            sums[flip(r), side, core] = folded(r).astype(BF16)
+            sums[flip(r), core] = folded(r).astype(BF16)
             fold_line(r, r & -r).start()
             if r == order[-2]:
+                relay(2, middle_term, middle_parts, middle_send_on, middle_recv_on)
                 relay(3, fine_term, fine_parts, fine_send_on, fine_recv_on)
         else:
             coarse_total[...] = folded(0).astype(BF16)
@@ -600,29 +609,41 @@
     group_spread(*coarse_trade)
     coarse_parts[group] = coarse_total[...]
 
+    def add_back(dy, da, piece):
+        for o in range(outer):
+            columns_of = pl.ds(pl.multiple_of((o * sides + quad_side(da)) * span, span), span)
+            total[:, columns_of] += piece[:, o * span : (o + 1) * span]
+
     @pl.when(first)
     def _():
-        tokens_grad[...] = total[...].astype(BF16)
-        back.wait_send()
+        add_back(0, 0, dot_transposed(act_take[0, 0], coarse_of(block_of(0, 0))))
+        for dy, da in peers:
+            if dy == 0:
+                quad_wait(3, back_give.at[0, 0], back_take, dy, da)
+                add_back(dy, da, back_take[dy, da].astype(F32))
+        for dy, da in peers:
+            back_copy(dy, da).wait_send()
 
     @pl.when(slot == 1)
     def _():
-        back.wait_recv()
-        tokens_grad[...] = (total[...] + back_take[...].astype(F32)).astype(BF16)
-
+        for dy, da in peers:
+            if dy:
+                quad_wait(3, back_give.at[0, 0], back_take, dy, da)
+                add_back(dy, da, back_take[dy, da].astype(F32))
+
+    tokens_grad[...] = total[...].astype(BF16)
     outs[1].start()
     pltpu.make_async_copy(others, others, path_send).wait()
-    for copy in (tokens_pair, pre_pair, act_pair):
-        copy.wait_send()
+    for dy, da in peers:
+        doc_copy(dy, da).wait_send()
+        quad_copy(1, pre_give.at[dy, da], pre_take, dy, da).wait_send()
+        quad_copy(2, act_give if dy else act_keep, act_take, dy, da).wait_send()
     for r in range(outer):
         for bit in gather_on(r):
             gather_copy(r, bit).wait_send()
-        for step in range(1, sides):
-            side_copy(r, step, True).wait_send()
-            fold_side(r, step).wait_send()
-        if cores > 1:
-            core_copy(r, True).wait_send()
-            fold_core(r).wait_send()
+        for step in range(1, cores):
+            core_copy(r, step, True).wait_send()
+            fold_core(r, step).wait_send()
         if r:
             fold_line(r, r & -r).wait_send()
     left(0, middle_send)
@@ -646,7 +667,9 @@
     medium, narrow = middle_w.shape[2], fine_w.shape[2]
     token_count, width = tokens.shape
     count = groups * members
-    outer, sides, cores = plan(groups, members, wide)
+    outer, sides, cores = plan(members, rows)
+    span = cores * rows
+    depth = outer * span
     steps = max(len(bits_of(outer)), 1)
     columns = wide // 2
 
@@ -675,9 +698,9 @@
             stack(groups, members, rows, narrow),
             stack(groups, blocks, rows, columns),
             pltpu.SMEM((count,) + path.shape, jnp.int32),
-            stack(2, *tokens.shape),
-            stack(*tokens.shape),
-            stack(blocks, outer, sides, cores, rows, columns),
+            stack(2, outer, sides, token_count, span),
+            stack(2, sides, outer, token_count, span),
+            stack(blocks, outer, cores, rows, columns),
             stack(*middle_w.shape),
             stack(*fine_w.shape),
             stack(members, rows, medium),
@@ -688,20 +711,20 @@
             stack(members, rows, narrow),
             stack(members, rows, medium),
             stack(members, rows, narrow),
-            stack(outer, sides, cores, blocks, rows, columns),
-            stack(outer, sides, blocks, rows, columns),
-            stack(outer, sides, blocks, rows, columns),
+            stack(outer, cores, blocks, rows, columns),
+            stack(outer, cores, blocks, rows, columns),
             stack(outer, steps, blocks, rows, columns),
             stack(blocks, rows, columns),
             stack(2, width, token_count),
-            stack(width, 2 * token_count),
+            stack(depth, 2 * sides * token_count),
             pltpu.VMEM((token_count, width), F32),
-            pltpu.VMEM((token_count, columns), F32),
-            pltpu.VMEM((token_count, columns), F32),
+            stack(2, sides, token_count, columns),
+            stack(2, sides, token_count, columns),
             stack(token_count, columns),
             stack(token_count, columns),
-            stack(token_count, width),
-            stack(token_count, width),
+            stack(2, sides, token_count, columns),
+            stack(2, sides, token_count, depth),
+            stack(2, sides, token_count, depth),
             pltpu.SemaphoreType.DMA,
             pltpu.SemaphoreType.DMA,
             sems(4),
@@ -709,18 +732,17 @@
             sems(2),
             sems(2, groups),
             sems(2, groups),
-            sems(4),
-            sems(4),
+            sems(4, 2, sides),
+            sems(4, 2, sides),
             sems(outer, steps),
             sems(outer),
-            sems(2, outer, sides),
-            sems(2, outer, sides),
-            sems(2, outer),
-            sems(2, outer),
+            sems(2, outer, cores),
+            sems(2, outer, cores),
             sems(outer),
             sems(outer, steps),
             sems(1),
-            sems(5),
+            sems(3),
+            sems(2, outer * sides),
             sems(5),
             pltpu.SemaphoreType.DMA,
             pltpu.SemaphoreType.DMA,

time: 77.3 us -> 81.9 us (1.060)
  Pallas kernels: 75.6 us -> 80.9 us
    pallas_call x1, Pallas kernels: 70.7 us -> 76 us  [exchange(): pl.pallas_call(functools.partial(main_kernel, groups, members), out_shape...]
where the time goes in v3:
time: 81.9 us; the launch traced here: 81.6 us
  Pallas kernels  80.9 us (99%)
    pallas_call x1, Pallas kernels, exchange(): pl.pallas_call(functools.partial(main_kernel, groups, members), out_shape...  76 us
    pallas_call x1, Pallas kernels, collect(): pl.pallas_call(collect_kernel, out_shape=tuple((jax.ShapeDtypeStruct(shap...  4.89 us

profile of v3, /device:TPU:0, one launch (start us, length us, event | category | flops | bytes accessed | tf_op | source)
XLA Modules:
  0.0 81.6 jit_solution(16541510912186790604)
XLA Ops:
  0.6 76.0 %exchange.1 = (s32[32,1,3]{2,1,0:T(1,128)}, bf16[128,1024]{1,0:T(8,128)(2,1)}, bf16[2,16,64,256]{3,2,1,0:T(8,128)(2,1)}, bf16[2,16,64,128]{3,2,1,0:T(8,128)(2,1)}, bf16[2,4,64,256]{3,2,1,0:T(8,128)(2,1)}) custom-call(s32[1,3]{1,0:T(1,128)} %path_row.1, bf16[128,1024]{1,0:T(8,128)(2,1)} %tokens_hbm.1, bf16[128,1024]{1,0:T(8,128)(2,1)} %cotangent_hbm.1, ...), custom_call_target="tpu_custom_call" | custom-call | tf_op jit(solution)/shard_map/exchange/pallas_call | solution.py:683
  76.7 4.9 %collect.1 = (bf16[128,1024]{1,0:T(8,128)(2,1)}, bf16[4,64,512]{2,1,0:T(8,128)(2,1)}, bf16[64,64,256]{2,1,0:T(8,128)(2,1)}, bf16[32,64,128]{2,1,0:T(8,128)(2,1)}) custom-call(s32[32,1,3]{2,1,0:T(1,128)} %get-tuple-element.9.path, s32[1]{0:T(128)} %bitcast.first_owned, bf16[128,1024]{1,0:T(8,128)(2,1)} %get-tuple-element.10.tokens_in, ...), custom_call_target="tpu_custom_call" | custom-call | tf_op jit(solution)/shard_map/collect/pallas_call | solution.py:834

commit v4 on v2

--- a/solution.py
+++ b/solution.py
@@ -188,9 +188,9 @@
         pltpu.make_async_copy(source, target, load_sem.at[index])
         for index, (source, target) in enumerate(
             (
+                (coarse_hbm.at[:, :, half], coarse_w.at[:, line, side, core]),
                 (tokens_hbm, both.at[0]),
                 (cotangent_hbm, both.at[1]),
-                (coarse_hbm.at[:, :, half], coarse_w.at[:, line, side, core]),
                 (fine_hbm, fine_w),
                 (middle_hbm, middle_w),
             )
@@ -221,8 +221,7 @@
         pl.semaphore_signal(barrier, inc=1, device_id=where, device_id_type=MESH)
 
     loop(1, count, greet)
-    for load in loads[:3]:
-        load.wait()
+    loads[0].wait()
     pl.semaphore_wait(barrier, count - 1)
 
     def path_copy(step):
@@ -298,6 +297,8 @@
             core_copy(r, True).start()
 
     pass_on(0)
+    for load in loads[1:3]:
+        load.wait()
     tokens_pair.start()
     for which in range(2):
         for start in range(0, width, LANES):
@@ -429,7 +430,7 @@
         return coarse_w[k].reshape(width, columns)
 
     first = slot == 0
-    pre_give[...] = dot(other_doc[...], coarse_of(other_block))
+    pre_give[...] = dot(other_doc[...], coarse_of(other_block)).astype(BF16)
     pre_pair = pair_copy(1, pre_give, pre_take)
     pre_pair.start()
     pre_own = dot(both[slot], coarse_of(own_block))
@@ -449,7 +450,7 @@
     middle_parts[group, me] = middle_term[me]
 
     pre_pair.wait_recv()
-    pre_other = pre_take[...]
+    pre_other = pre_take[...].astype(F32)
     hidden, before_grad = gelu_parts(
         jnp.where(first, pre_own, pre_other), jnp.where(first, pre_other, pre_own)
     )
@@ -463,6 +464,11 @@
     def _():
         total[...] += dot_transposed(act_own, coarse_of(own_block))
 
+    arrive(1, fine_block)
+    total[...] += compute(fine_block, fine_term)
+    spread(3, fine_term, fine_own)
+    fine_parts[group, me] = fine_term[me]
+
     act_pair.wait_recv()
     act_other = act_take[...]
     back = pair_copy(3, back_give, back_take)
@@ -473,7 +479,7 @@
         value = dot(pair_t[...], jnp.concatenate([mine, theirs], axis=0))
         sums[:, :, :, k] = value.astype(BF16).reshape(outer, sides, cores, rows, columns)
 
-    order = list(range(outer - 1, 0, -2)) + list(range(outer - 2, 0, -2)) + [0]
+    order = list(range(outer - 1, -1, -1))
 
     def fold_core(r):
         return to_member(
@@ -534,11 +540,6 @@
                 ).astype(BF16)
         for step in range(1, sides):
             fold_side(r, step).start()
-
-    arrive(1, fine_block)
-    total[...] += compute(fine_block, fine_term)
-    spread(3, fine_term, fine_own)
-    fine_parts[group, me] = fine_term[me]
 
     def hand_on(target, send_on, recv_on, p, step, landing_own):
         other = lax.rem(group + step, groups)
@@ -696,8 +697,8 @@
             stack(2, width, token_count),
             stack(width, 2 * token_count),
             pltpu.VMEM((token_count, width), F32),
-            pltpu.VMEM((token_count, columns), F32),
-            pltpu.VMEM((token_count, columns), F32),
+            stack(token_count, columns),
+            stack(token_count, columns),
             stack(token_count, columns),
             stack(token_count, columns),
             stack(token_count, width),
@@ -735,16 +736,21 @@
 
 
 def collect_kernel(
-    path,
-    first_owned,
-    tokens_in,
+    path_hbm,
+    tokens_hbm,
     middle_hbm,
     fine_hbm,
-    coarse_parts,
+    coarse_hbm,
+    tokens_out,
+    coarse_out,
+    middle_out,
+    fine_out,
+    path,
     tokens_grad,
     coarse_grad,
     middle_grad,
     fine_grad,
+    coarse_parts,
     middle_parts,
     fine_parts,
     middle_sum,
@@ -752,27 +758,73 @@
     middle_last,
     fine_last,
     load_sem,
+    out_sem,
 ):
     count = middle_parts.shape[0]
     owned = fine_grad.shape[0]
-    loads = (
-        pltpu.make_async_copy(middle_hbm, middle_parts, load_sem.at[0]),
-        pltpu.make_async_copy(fine_hbm, fine_parts, load_sem.at[1]),
-    )
+    first_owned = lax.axis_index("grp") * owned
+    loads = [
+        pltpu.make_async_copy(source, target, load_sem.at[index])
+        for index, (source, target) in enumerate(
+            (
+                (path_hbm, path),
+                (middle_hbm, middle_parts),
+                (fine_hbm, fine_parts),
+                (coarse_hbm, coarse_parts),
+                (tokens_hbm, tokens_grad),
+            )
+        )
+    ]
+    outs = [
+        pltpu.make_async_copy(source, target, out_sem.at[index])
+        for index, (source, target) in enumerate(
+            (
+                (tokens_grad, tokens_out),
+                (coarse_grad, coarse_out),
+                (middle_grad, middle_out),
+                (fine_grad, fine_out),
+            )
+        )
+    ]
     for load in loads:
         load.start()
+    for last in (middle_last, fine_last):
+        for k in range(last.shape[0]):
+            last[k] = count
     middle_grad[...] = jnp.zeros_like(middle_grad)
-    fine_grad[...] = jnp.zeros_like(fine_grad)
     middle_sum[count] = jnp.zeros(middle_sum.shape[1:], F32)
     fine_sum[count] = jnp.zeros(fine_sum.shape[1:], F32)
-    for last in (middle_last, fine_last):
-
-        def clear(k, carry, last=last):
-            last[k] = count
-            return carry
-
-        lax.fori_loop(0, last.shape[0], clear, 0)
-    tokens_grad[...] = tokens_in[...]
+    loads[0].wait()
+    loads[1].wait()
+
+    def add_middle(document, carry):
+        k = path[document, 0, 1]
+        value = middle_parts[document].astype(F32) + middle_sum[middle_last[k]]
+        middle_sum[document] = value
+        middle_grad[k] = value.astype(BF16)
+        middle_last[k] = document
+        return carry
+
+    lax.fori_loop(0, count, add_middle, 0)
+    outs[2].start()
+    fine_grad[...] = jnp.zeros_like(fine_grad)
+    loads[2].wait()
+
+    def add_fine(document, carry):
+        place = path[document, 0, 2] - first_owned
+
+        @pl.when((place >= 0) & (place < owned))
+        def _():
+            piece = fine_parts[document].astype(F32) + fine_sum[fine_last[place]]
+            fine_sum[document] = piece
+            fine_grad[place] = piece.astype(BF16)
+            fine_last[place] = document
+
+        return carry
+
+    lax.fori_loop(0, count, add_fine, 0)
+    outs[3].start()
+    loads[3].wait()
     groups, _, _, columns = coarse_parts.shape
     team = coarse_grad.shape[2] // columns
     for s in range(team):
@@ -780,54 +832,39 @@
         for other in range(s + team, groups, team):
             value = value + coarse_parts[other].astype(F32)
         coarse_grad[:, :, s * columns : (s + 1) * columns] = value.astype(BF16)
-    for load in loads:
-        load.wait()
-
-    def add(document, carry):
-        k = path[document, 0, 1]
-        value = middle_parts[document].astype(F32) + middle_sum[middle_last[k]]
-        middle_sum[document] = value
-        middle_grad[k] = value.astype(BF16)
-        middle_last[k] = document
-        place = path[document, 0, 2] - first_owned[0]
-
-        @pl.when((place >= 0) & (place < owned))
-        def _():
-            piece = fine_parts[document].astype(F32) + fine_sum[fine_last[place]]
-            fine_sum[document] = piece
-            fine_grad[place] = piece.astype(BF16)
-            fine_last[place] = document
-
-        return carry
-
-    lax.fori_loop(0, count, add, 0)
-
-
-def collect(paths, first_owned, tokens_grad, middle_parts, fine_parts, coarse_parts, shapes):
-    vmem = pl.BlockSpec(memory_space=pltpu.VMEM)
-    smem = pl.BlockSpec(memory_space=pltpu.SMEM)
+    outs[1].start()
+    loads[4].wait()
+    outs[0].start()
+    for out in outs:
+        out.wait()
+
+
+def collect(paths, tokens_grad, middle_parts, fine_parts, coarse_parts, shapes):
     hbm = pl.BlockSpec(memory_space=pl.ANY)
     count, rows, medium = middle_parts.shape
     narrow = fine_parts.shape[2]
+    outs = (tokens_grad.shape,) + shapes
     return pl.pallas_call(
         collect_kernel,
-        out_shape=tuple(
-            jax.ShapeDtypeStruct(shape, BF16) for shape in (tokens_grad.shape,) + shapes
-        ),
-        in_specs=[smem, smem, vmem, hbm, hbm, vmem],
-        out_specs=(vmem,) * 4,
-        scratch_shapes=[
+        out_shape=tuple(jax.ShapeDtypeStruct(shape, BF16) for shape in outs),
+        in_specs=[hbm] * 5,
+        out_specs=(hbm,) * 4,
+        scratch_shapes=[pltpu.SMEM(paths.shape, jnp.int32)]
+        + [pltpu.VMEM(shape, BF16) for shape in outs]
+        + [
+            pltpu.VMEM(coarse_parts.shape, BF16),
             pltpu.VMEM(middle_parts.shape, BF16),
             pltpu.VMEM(fine_parts.shape, BF16),
             pltpu.VMEM((count + 1, rows, medium), F32),
             pltpu.VMEM((count + 1, rows, narrow), F32),
             pltpu.SMEM((shapes[1][0],), jnp.int32),
             pltpu.SMEM((shapes[2][0],), jnp.int32),
-            pltpu.SemaphoreType.DMA((2,)),
+            pltpu.SemaphoreType.DMA((5,)),
+            pltpu.SemaphoreType.DMA((4,)),
         ],
         compiler_params=pltpu.CompilerParams(vmem_limit_bytes=60 * 2**20),
         name="collect",
-    )(paths, first_owned, tokens_grad, middle_parts, fine_parts, coarse_parts)
+    )(paths, tokens_grad, middle_parts, fine_parts, coarse_parts)
 
 
 def on_device(tokens, cotangent, path, coarse_weights, middle_weights, fine_weights):
@@ -836,11 +873,9 @@
     paths, tokens_grad, middle_parts, fine_parts, coarse_parts = exchange(
         path, tokens, cotangent, coarse_weights, middle_weights, fine_weights, groups, members
     )
-    first_owned = (lax.axis_index("grp") * fine_weights.shape[0]).astype(jnp.int32).reshape(1)
     flat = lambda parts: parts.reshape((groups * members,) + parts.shape[2:])
     return collect(
         paths,
-        first_owned,
         tokens_grad,
         flat(middle_parts),
         flat(fine_parts),

time: 77.3 us -> 74 us (0.957)
  Pallas kernels: 75.6 us -> 72.4 us
    pallas_call x1, Pallas kernels: 70.7 us -> 68.8 us  [exchange(): pl.pallas_call(functools.partial(main_kernel, groups, members), out_shape...]
    pallas_call x1, Pallas kernels: 4.88 us -> 3.54 us  [collect(): pl.pallas_call(collect_kernel, out_shape=tuple((jax.ShapeDtypeStruct(shap...]
where the time goes in v4:
time: 74 us; the launch traced here: 73 us
  Pallas kernels  72.4 us (98%)
    pallas_call x1, Pallas kernels, exchange(): pl.pallas_call(functools.partial(main_kernel, groups, members), out_shape...  68.8 us
    pallas_call x1, Pallas kernels, collect(): pl.pallas_call(collect_kernel, out_shape=tuple((jax.ShapeDtypeStruct(shap...  3.54 us

profile of v4, /device:TPU:0, one launch (start us, length us, event | category | flops | bytes accessed | tf_op | source)
XLA Modules:
  0.0 73.0 jit_solution(8614699010700141920)
XLA Ops:
  0.6 68.8 %exchange.1 = (s32[32,1,3]{2,1,0:T(1,128)}, bf16[128,1024]{1,0:T(8,128)(2,1)}, bf16[2,16,64,256]{3,2,1,0:T(8,128)(2,1)}, bf16[2,16,64,128]{3,2,1,0:T(8,128)(2,1)}, bf16[2,4,64,256]{3,2,1,0:T(8,128)(2,1)}) custom-call(s32[1,3]{1,0:T(1,128)} %path_row.1, bf16[128,1024]{1,0:T(8,128)(2,1)} %tokens_hbm.1, bf16[128,1024]{1,0:T(8,128)(2,1)} %cotangent_hbm.1, ...), custom_call_target="tpu_custom_call" | custom-call | tf_op jit(solution)/shard_map/exchange/pallas_call | solution.py:661
  69.5 3.5 %collect.1 = (bf16[128,1024]{1,0:T(8,128)(2,1)}, bf16[4,64,512]{2,1,0:T(8,128)(2,1)}, bf16[64,64,256]{2,1,0:T(8,128)(2,1)}, bf16[32,64,128]{2,1,0:T(8,128)(2,1)}) custom-call(s32[32,1,3]{2,1,0:T(1,128)} %get-tuple-element.9.path_hbm, bf16[128,1024]{1,0:T(8,128)(2,1)} %get-tuple-element.10.tokens_hbm, bf16[32,64,256]{2,1,0:T(8,128)(2,1)} %bitcast.2, ...), custom_call_target="tpu_custom_call" | custom-call | tf_op jit(solution)/shard_map/collect/pallas_call | solution.py:847

commit v5 on v3

--- a/solution.py
+++ b/solution.py
@@ -155,8 +155,9 @@
     place = lax.rem(me, inner)
     side = place // cores
     core = lax.rem(place, cores)
-    slot = lax.rem(group, 2)
-    mirror = group + 1 - 2 * slot
+    twist = 1 - sides % 2
+    slot = lax.rem(group + twist * side, 2)
+    mirror = group + 1 - 2 * lax.rem(group, 2)
     width = tokens_grad.shape[1]
 
     def loop(start, stop, body):
@@ -255,6 +256,9 @@
     quad = [(dy, da) for dy in range(2) for da in range(sides)]
     peers = quad[1:]
 
+    def differs(dy, da):
+        return (dy + twist * da) % 2
+
     def quad_side(da):
         return lax.rem(side + da, sides)
 
@@ -272,25 +276,17 @@
     def quad_wait(stage, source, target, dy, da):
         quad_copy(stage, source, target, dy, (sides - da) % sides).wait_recv()
 
-    def gather_copy(r, bit):
-        piece = coarse_w.at[:, flip(r), core]
+    def gather_copy(r):
+        piece = coarse_w.at[:, line, core]
         return to_member(
-            piece,
-            piece,
-            gather_send.at[r, bits.index(bit)],
-            gather_recv.at[r ^ bit],
-            at_line(bit, side, core),
+            piece, piece, gather_send.at[r, 0], gather_recv.at[r], at_line(r, side, core)
         )
 
     def gather_wait(r):
         piece = coarse_w.at[:, flip(r), core]
-        bit = r & -r
         to_member(
-            piece, piece, gather_send.at[0, 0], gather_recv.at[r], at_line(bit, side, core)
+            piece, piece, gather_send.at[r, 0], gather_recv.at[r], at_line(r, side, core)
         ).wait_recv()
-
-    def gather_on(r):
-        return [bit for bit in bits if r == 0 or bit < (r & -r)]
 
     def core_copy(r, step, landing_own):
         there = lax.rem(core + step, cores)
@@ -301,13 +297,14 @@
         )
 
     def pass_on(r):
-        for bit in gather_on(r):
-            gather_copy(r, bit).start()
+        if r == 0:
+            for far in range(outer - 1, 0, -1):
+                gather_copy(far).start()
         for step in range(1, cores):
             core_copy(r, step, True).start()
 
     def doc_copy(dy, da):
-        which = 1 - slot if dy else slot
+        which = 1 - slot if differs(dy, da) else slot
         return quad_copy(0, both.at[which, :, quad_side(da)], docs, dy, da)
 
     pass_on(0)
@@ -421,15 +418,6 @@
         quad_wait(0, both.at[0, :, 0], docs, dy, da)
         turn(dy, da)
 
-    def merge_fine(p):
-        owner = route(group * members + p, 2) // owned
-        fine_send[p] = fine_in[owner, p]
-
-    group_arrive(*fine_trade)
-    loop(0, members, merge_fine)
-    spread(1, fine_send, fine_block)
-    fine_block[me] = fine_send[me]
-
     for r in range(3, outer, 2):
         gather_wait(r)
         pass_on(r)
@@ -451,6 +439,15 @@
     for dy, da in peers:
         pre_give[dy, da] = dot(wide_of(dy, da), coarse_of(block_of(dy, da))).astype(BF16)
         quad_copy(1, pre_give.at[dy, da], pre_take, dy, da).start()
+    def merge_fine(p):
+        owner = route(group * members + p, 2) // owned
+        fine_send[p] = fine_in[owner, p]
+
+    group_arrive(*fine_trade)
+    loop(0, members, merge_fine)
+    spread(1, fine_send, fine_block)
+    fine_block[me] = fine_send[me]
+
     pre_own = dot(wide_of(0, 0), coarse_of(block_of(0, 0)))
     pre_other = jnp.zeros_like(pre_own)
 
@@ -469,7 +466,7 @@
     for dy, da in peers:
         quad_wait(1, pre_give.at[0, 0], pre_take, dy, da)
     for dy, da in peers:
-        if dy:
+        if differs(dy, da):
             pre_other = pre_other + pre_take[dy, da].astype(F32)
         else:
             pre_own = pre_own + pre_take[dy, da].astype(F32)
@@ -481,7 +478,7 @@
     act_keep[...] = jnp.where(first, before_grad, hidden).astype(BF16)
     act_take[0, 0] = act_keep[...]
     for dy, da in peers:
-        quad_copy(2, act_give if dy else act_keep, act_take, dy, da).start()
+        quad_copy(2, act_give if differs(dy, da) else act_keep, act_take, dy, da).start()
 
     arrive(0, middle_block)
     total[...] = compute(middle_block, middle_term)
@@ -564,19 +561,20 @@
             device_id_type=MESH,
         )
 
-    def relay(index, source, target, send_on, recv_on):
+    def relay(index, source, target, send_on, recv_on, first_step=0, last_step=members):
         own = target.at[group]
 
         def start(p):
             loop(1, groups, lambda step: hand_on(target, send_on, recv_on, p, step, True).start())
 
         def body(step):
-            p = lax.rem(me + members - step, members)
+            p = partner(step)
             member_copy(index, source, own, p, False).wait_recv()
             start(p)
 
-        start(me)
-        loop(1, members, body)
+        if first_step == 0:
+            start(me)
+        loop(max(first_step, 1), last_step, body)
 
     def relay_done(target, send_on, recv_on):
         if groups > 1:
@@ -591,6 +589,7 @@
             value = value + from_line[r, bits.index(bit)].astype(F32)
         return value
 
+    relay(2, middle_term, middle_parts, middle_send_on, middle_recv_on, 0, near)
     for r in order:
         for step in range(1, cores):
             fold_core(r, step).wait_recv()
@@ -599,8 +598,9 @@
         if r:
             sums[flip(r), core] = folded(r).astype(BF16)
             fold_line(r, r & -r).start()
+            if r == 1:
+                relay(2, middle_term, middle_parts, middle_send_on, middle_recv_on, near, members)
             if r == order[-2]:
-                relay(2, middle_term, middle_parts, middle_send_on, middle_recv_on)
                 relay(3, fine_term, fine_parts, fine_send_on, fine_recv_on)
         else:
             coarse_total[...] = folded(0).astype(BF16)
@@ -618,7 +618,7 @@
     def _():
         add_back(0, 0, dot_transposed(act_take[0, 0], coarse_of(block_of(0, 0))))
         for dy, da in peers:
-            if dy == 0:
+            if not differs(dy, da):
                 quad_wait(3, back_give.at[0, 0], back_take, dy, da)
                 add_back(dy, da, back_take[dy, da].astype(F32))
         for dy, da in peers:
@@ -627,7 +627,7 @@
     @pl.when(slot == 1)
     def _():
         for dy, da in peers:
-            if dy:
+            if differs(dy, da):
                 quad_wait(3, back_give.at[0, 0], back_take, dy, da)
                 add_back(dy, da, back_take[dy, da].astype(F32))
 
@@ -637,10 +637,10 @@
     for dy, da in peers:
         doc_copy(dy, da).wait_send()
         quad_copy(1, pre_give.at[dy, da], pre_take, dy, da).wait_send()
-        quad_copy(2, act_give if dy else act_keep, act_take, dy, da).wait_send()
+        quad_copy(2, act_give if differs(dy, da) else act_keep, act_take, dy, da).wait_send()
     for r in range(outer):
-        for bit in gather_on(r):
-            gather_copy(r, bit).wait_send()
+        if r:
+            gather_copy(r).wait_send()
         for step in range(1, cores):
             core_copy(r, step, True).wait_send()
             fold_core(r, step).wait_send()
@@ -757,16 +757,21 @@
 
 
 def collect_kernel(
-    path,
-    first_owned,
-    tokens_in,
+    path_hbm,
+    tokens_hbm,
     middle_hbm,
     fine_hbm,
-    coarse_parts,
+    coarse_hbm,
+    tokens_out,
+    coarse_out,
+    middle_out,
+    fine_out,
+    path,
     tokens_grad,
     coarse_grad,
     middle_grad,
     fine_grad,
+    coarse_parts,
     middle_parts,
     fine_parts,
     middle_sum,
@@ -774,44 +779,60 @@
     middle_last,
     fine_last,
     load_sem,
+    out_sem,
 ):
     count = middle_parts.shape[0]
     owned = fine_grad.shape[0]
-    loads = (
-        pltpu.make_async_copy(middle_hbm, middle_parts, load_sem.at[0]),
-        pltpu.make_async_copy(fine_hbm, fine_parts, load_sem.at[1]),
-    )
+    first_owned = lax.axis_index("grp") * owned
+    loads = [
+        pltpu.make_async_copy(source, target, load_sem.at[index])
+        for index, (source, target) in enumerate(
+            (
+                (path_hbm, path),
+                (middle_hbm, middle_parts),
+                (fine_hbm, fine_parts),
+                (coarse_hbm, coarse_parts),
+                (tokens_hbm, tokens_grad),
+            )
+        )
+    ]
+    outs = [
+        pltpu.make_async_copy(source, target, out_sem.at[index])
+        for index, (source, target) in enumerate(
+            (
+                (tokens_grad, tokens_out),
+                (coarse_grad, coarse_out),
+                (middle_grad, middle_out),
+                (fine_grad, fine_out),
+            )
+        )
+    ]
     for load in loads:
         load.start()
+    for last in (middle_last, fine_last):
+        for k in range(last.shape[0]):
+            last[k] = count
     middle_grad[...] = jnp.zeros_like(middle_grad)
-    fine_grad[...] = jnp.zeros_like(fine_grad)
     middle_sum[count] = jnp.zeros(middle_sum.shape[1:], F32)
     fine_sum[count] = jnp.zeros(fine_sum.shape[1:], F32)
-    for last in (middle_last, fine_last):
-
-        def clear(k, carry, last=last):
-            last[k] = count
-            return carry
-
-        lax.fori_loop(0, last.shape[0], clear, 0)
-    tokens_grad[...] = tokens_in[...]
-    groups, _, _, columns = coarse_parts.shape
-    team = coarse_grad.shape[2] // columns
-    for s in range(team):
-        value = coarse_parts[s].astype(F32)
-        for other in range(s + team, groups, team):
-            value = value + coarse_parts[other].astype(F32)
-        coarse_grad[:, :, s * columns : (s + 1) * columns] = value.astype(BF16)
-    for load in loads:
-        load.wait()
-
-    def add(document, carry):
+    loads[0].wait()
+    loads[1].wait()
+
+    def add_middle(document, carry):
         k = path[document, 0, 1]
         value = middle_parts[document].astype(F32) + middle_sum[middle_last[k]]
         middle_sum[document] = value
         middle_grad[k] = value.astype(BF16)
         middle_last[k] = document
-        place = path[document, 0, 2] - first_owned[0]
+        return carry
+
+    lax.fori_loop(0, count, add_middle, 0)
+    outs[2].start()
+    fine_grad[...] = jnp.zeros_like(fine_grad)
+    loads[2].wait()
+
+    def add_fine(document, carry):
+        place = path[document, 0, 2] - first_owned
 
         @pl.when((place >= 0) & (place < owned))
         def _():
@@ -822,34 +843,51 @@
 
         return carry
 
-    lax.fori_loop(0, count, add, 0)
-
-
-def collect(paths, first_owned, tokens_grad, middle_parts, fine_parts, coarse_parts, shapes):
-    vmem = pl.BlockSpec(memory_space=pltpu.VMEM)
-    smem = pl.BlockSpec(memory_space=pltpu.SMEM)
+    lax.fori_loop(0, count, add_fine, 0)
+    outs[3].start()
+    loads[3].wait()
+    groups, _, _, columns = coarse_parts.shape
+    outer, sides, cores = plan(lax.axis_size("mem"), coarse_grad.shape[1])
+    side = lax.rem(lax.axis_index("mem"), sides * cores) // cores
+    for s in range(2):
+        held = lax.rem(s + (1 - sides % 2) * side, 2)
+        value = coarse_parts[held].astype(F32)
+        for other in range(2, groups, 2):
+            value = value + coarse_parts[held + other].astype(F32)
+        coarse_grad[:, :, s * columns : (s + 1) * columns] = value.astype(BF16)
+    outs[1].start()
+    loads[4].wait()
+    outs[0].start()
+    for out in outs:
+        out.wait()
+
+
+def collect(paths, tokens_grad, middle_parts, fine_parts, coarse_parts, shapes):
     hbm = pl.BlockSpec(memory_space=pl.ANY)
     count, rows, medium = middle_parts.shape
     narrow = fine_parts.shape[2]
+    outs = (tokens_grad.shape,) + shapes
     return pl.pallas_call(
         collect_kernel,
-        out_shape=tuple(
-            jax.ShapeDtypeStruct(shape, BF16) for shape in (tokens_grad.shape,) + shapes
-        ),
-        in_specs=[smem, smem, vmem, hbm, hbm, vmem],
-        out_specs=(vmem,) * 4,
-        scratch_shapes=[
+        out_shape=tuple(jax.ShapeDtypeStruct(shape, BF16) for shape in outs),
+        in_specs=[hbm] * 5,
+        out_specs=(hbm,) * 4,
+        scratch_shapes=[pltpu.SMEM(paths.shape, jnp.int32)]
+        + [pltpu.VMEM(shape, BF16) for shape in outs]
+        + [
+            pltpu.VMEM(coarse_parts.shape, BF16),
             pltpu.VMEM(middle_parts.shape, BF16),
             pltpu.VMEM(fine_parts.shape, BF16),
             pltpu.VMEM((count + 1, rows, medium), F32),
             pltpu.VMEM((count + 1, rows, narrow), F32),
             pltpu.SMEM((shapes[1][0],), jnp.int32),
             pltpu.SMEM((shapes[2][0],), jnp.int32),
-            pltpu.SemaphoreType.DMA((2,)),
+            pltpu.SemaphoreType.DMA((5,)),
+            pltpu.SemaphoreType.DMA((4,)),
         ],
         compiler_params=pltpu.CompilerParams(vmem_limit_bytes=60 * 2**20),
         name="collect",
-    )(paths, first_owned, tokens_grad, middle_parts, fine_parts, coarse_parts)
+    )(paths, tokens_grad, middle_parts, fine_parts, coarse_parts)
 
 
 def on_device(tokens, cotangent, path, coarse_weights, middle_weights, fine_weights):
@@ -858,11 +896,9 @@
     paths, tokens_grad, middle_parts, fine_parts, coarse_parts = exchange(
         path, tokens, cotangent, coarse_weights, middle_weights, fine_weights, groups, members
     )
-    first_owned = (lax.axis_index("grp") * fine_weights.shape[0]).astype(jnp.int32).reshape(1)
     flat = lambda parts: parts.reshape((groups * members,) + parts.shape[2:])
     return collect(
         paths,
-        first_owned,
         tokens_grad,
         flat(middle_parts),
         flat(fine_parts),

time: 81.9 us -> 73.2 us (0.89)
  Pallas kernels: 80.9 us -> 71.5 us
    pallas_call x1, Pallas kernels: 76 us -> 68 us  [exchange(): pl.pallas_call(functools.partial(main_kernel, groups, members), out_shape...]
    pallas_call x1, Pallas kernels: 4.89 us -> 3.54 us  [collect(): pl.pallas_call(collect_kernel, out_shape=tuple((jax.ShapeDtypeStruct(shap...]
where the time goes in v5:
time: 73.2 us; the launch traced here: 72.1 us
  Pallas kernels  71.5 us (98%)
    pallas_call x1, Pallas kernels, exchange(): pl.pallas_call(functools.partial(main_kernel, groups, members), out_shape...  68 us
    pallas_call x1, Pallas kernels, collect(): pl.pallas_call(collect_kernel, out_shape=tuple((jax.ShapeDtypeStruct(shap...  3.54 us

profile of v5, /device:TPU:0, one launch (start us, length us, event | category | flops | bytes accessed | tf_op | source)
XLA Modules:
  0.0 72.1 jit_solution(2825994782592421140)
XLA Ops:
  0.6 68.0 %exchange.1 = (s32[32,1,3]{2,1,0:T(1,128)}, bf16[128,1024]{1,0:T(8,128)(2,1)}, bf16[2,16,64,256]{3,2,1,0:T(8,128)(2,1)}, bf16[2,16,64,128]{3,2,1,0:T(8,128)(2,1)}, bf16[2,4,64,256]{3,2,1,0:T(8,128)(2,1)}) custom-call(s32[1,3]{1,0:T(1,128)} %path_row.1, bf16[128,1024]{1,0:T(8,128)(2,1)} %tokens_hbm.1, bf16[128,1024]{1,0:T(8,128)(2,1)} %cotangent_hbm.1, ...), custom_call_target="tpu_custom_call" | custom-call | tf_op jit(solution)/shard_map/exchange/pallas_call | solution.py:683
  68.6 3.5 %collect.1 = (bf16[128,1024]{1,0:T(8,128)(2,1)}, bf16[4,64,512]{2,1,0:T(8,128)(2,1)}, bf16[64,64,256]{2,1,0:T(8,128)(2,1)}, bf16[32,64,128]{2,1,0:T(8,128)(2,1)}) custom-call(s32[32,1,3]{2,1,0:T(1,128)} %get-tuple-element.9.path_hbm, bf16[128,1024]{1,0:T(8,128)(2,1)} %get-tuple-element.10.tokens_hbm, bf16[32,64,256]{2,1,0:T(8,128)(2,1)} %bitcast.2, ...), custom_call_target="tpu_custom_call" | custom-call | tf_op jit(solution)/shard_map/collect/pallas_call | solution.py:870

commit v6 on v5

--- a/solution.py
+++ b/solution.py
@@ -203,7 +203,7 @@
         pltpu.make_async_copy(
             source.at[:, pl.ds(index * span, span)],
             both.at[which, o, a],
-            token_sem.at[which, index],
+            token_sem,
         )
         for which, source in enumerate((tokens_hbm, cotangent_hbm))
         for index, (o, a) in enumerate(places)
@@ -279,13 +279,13 @@
     def gather_copy(r):
         piece = coarse_w.at[:, line, core]
         return to_member(
-            piece, piece, gather_send.at[r, 0], gather_recv.at[r], at_line(r, side, core)
+            piece, piece, gather_send, gather_recv.at[r], at_line(r, side, core)
         )
 
     def gather_wait(r):
         piece = coarse_w.at[:, flip(r), core]
         to_member(
-            piece, piece, gather_send.at[r, 0], gather_recv.at[r], at_line(r, side, core)
+            piece, piece, gather_send, gather_recv.at[r], at_line(r, side, core)
         ).wait_recv()
 
     def core_copy(r, step, landing_own):
@@ -293,12 +293,12 @@
         landing = core if landing_own else lax.rem(core + cores - step, cores)
         piece = coarse_w.at[:, flip(r), landing]
         return to_member(
-            piece, piece, core_send.at[0, r, step], core_recv.at[0, r, step], at_line(0, side, there)
+            piece, piece, core_send.at[0, step], core_recv.at[0, r, step], at_line(0, side, there)
         )
 
     def pass_on(r):
         if r == 0:
-            for far in range(outer - 1, 0, -1):
+            for far in range(1, outer):
                 gather_copy(far).start()
         for step in range(1, cores):
             core_copy(r, step, True).start()
@@ -308,8 +308,7 @@
         return quad_copy(0, both.at[which, :, quad_side(da)], docs, dy, da)
 
     pass_on(0)
-    for load in token_loads:
-        load.wait()
+    pltpu.make_async_copy(both, both, token_sem).wait()
     for dy, da in peers:
         doc_copy(dy, da).start()
     for which in range(2):
@@ -508,7 +507,7 @@
         return to_member(
             sums.at[flip(r), there],
             from_core.at[r, step],
-            core_send.at[1, r, step],
+            core_send.at[1, step],
             core_recv.at[1, r, step],
             at_line(0, side, there),
         )
@@ -517,7 +516,7 @@
         return to_member(
             sums.at[flip(r), core],
             from_line.at[r ^ bit, bits.index(bit)],
-            fold_send.at[r],
+            fold_send,
             fold_recv.at[r ^ bit, bits.index(bit)],
             at_line(bit, side, core),
         )
@@ -526,7 +525,7 @@
         to_member(
             sums.at[flip(r), core],
             from_line.at[r, bits.index(bit)],
-            fold_send.at[r],
+            fold_send,
             fold_recv.at[r, bits.index(bit)],
             at_line(bit, side, core),
         ).wait_recv()
@@ -638,14 +637,16 @@
         doc_copy(dy, da).wait_send()
         quad_copy(1, pre_give.at[dy, da], pre_take, dy, da).wait_send()
         quad_copy(2, act_give if differs(dy, da) else act_keep, act_take, dy, da).wait_send()
-    for r in range(outer):
-        if r:
-            gather_copy(r).wait_send()
-        for step in range(1, cores):
-            core_copy(r, step, True).wait_send()
-            fold_core(r, step).wait_send()
-        if r:
-            fold_line(r, r & -r).wait_send()
+    for step in range(1, cores):
+        some = coarse_w.at[:, :, core]
+        pltpu.make_async_copy(some, some, core_send.at[0, step]).wait()
+        some = sums.at[:, core]
+        pltpu.make_async_copy(some, some, core_send.at[1, step]).wait()
+    if outer > 1:
+        some = coarse_w.at[:, pl.ds(0, outer - 1), core]
+        pltpu.make_async_copy(some, some, gather_send).wait()
+        some = sums.at[pl.ds(0, outer - 1), core]
+        pltpu.make_async_copy(some, some, fold_send).wait()
     left(0, middle_send)
     left(1, fine_send)
     group_left(*fine_trade)
@@ -734,15 +735,15 @@
             sems(2, groups),
             sems(4, 2, sides),
             sems(4, 2, sides),
-            sems(outer, steps),
+            pltpu.SemaphoreType.DMA,
             sems(outer),
+            sems(2, cores),
             sems(2, outer, cores),
-            sems(2, outer, cores),
-            sems(outer),
+            pltpu.SemaphoreType.DMA,
             sems(outer, steps),
             sems(1),
             sems(3),
-            sems(2, outer * sides),
+            pltpu.SemaphoreType.DMA,
             sems(5),
             pltpu.SemaphoreType.DMA,
             pltpu.SemaphoreType.DMA,

time: 73.2 us -> 72.2 us (0.986); the launches traced: 72.1 us -> 72 us
  no operation moved by 1% of the time
where the time goes in v6:
time: 72.2 us; the launch traced here: 72 us
  Pallas kernels  71.3 us (99%)
    pallas_call x1, Pallas kernels, exchange(): pl.pallas_call(functools.partial(main_kernel, groups, members), out_shape...  67.8 us
    pallas_call x1, Pallas kernels, collect(): pl.pallas_call(collect_kernel, out_shape=tuple((jax.ShapeDtypeStruct(shap...  3.54 us

profile of v6, /device:TPU:0, one launch (start us, length us, event | category | flops | bytes accessed | tf_op | source)
XLA Modules:
  0.0 72.0 jit_solution(17115121167822720543)
XLA Ops:
  0.6 67.8 %exchange.1 = (s32[32,1,3]{2,1,0:T(1,128)}, bf16[128,1024]{1,0:T(8,128)(2,1)}, bf16[2,16,64,256]{3,2,1,0:T(8,128)(2,1)}, bf16[2,16,64,128]{3,2,1,0:T(8,128)(2,1)}, bf16[2,4,64,256]{3,2,1,0:T(8,128)(2,1)}) custom-call(s32[1,3]{1,0:T(1,128)} %path_row.1, bf16[128,1024]{1,0:T(8,128)(2,1)} %tokens_hbm.1, bf16[128,1024]{1,0:T(8,128)(2,1)} %cotangent_hbm.1, ...), custom_call_target="tpu_custom_call" | custom-call | tf_op jit(solution)/shard_map/exchange/pallas_call | solution.py:684
  68.4 3.5 %collect.1 = (bf16[128,1024]{1,0:T(8,128)(2,1)}, bf16[4,64,512]{2,1,0:T(8,128)(2,1)}, bf16[64,64,256]{2,1,0:T(8,128)(2,1)}, bf16[32,64,128]{2,1,0:T(8,128)(2,1)}) custom-call(s32[32,1,3]{2,1,0:T(1,128)} %get-tuple-element.9.path_hbm, bf16[128,1024]{1,0:T(8,128)(2,1)} %get-tuple-element.10.tokens_hbm, bf16[32,64,256]{2,1,0:T(8,128)(2,1)} %bitcast.2, ...), custom_call_target="tpu_custom_call" | custom-call | tf_op jit(solution)/shard_map/collect/pallas_call | solution.py:871

commit v7 on v6

--- a/solution.py
+++ b/solution.py
@@ -484,11 +484,6 @@
     spread(2, middle_term, middle_own)
     middle_parts[group, me] = middle_term[me]
 
-    arrive(1, fine_block)
-    total[...] += compute(fine_block, fine_term)
-    spread(3, fine_term, fine_own)
-    fine_parts[group, me] = fine_term[me]
-
     for dy, da in peers:
         quad_wait(2, act_keep, act_take, dy, da)
 
@@ -587,6 +582,11 @@
         for bit in lower(r):
             value = value + from_line[r, bits.index(bit)].astype(F32)
         return value
+
+    arrive(1, fine_block)
+    total[...] += compute(fine_block, fine_term)
+    spread(3, fine_term, fine_own)
+    fine_parts[group, me] = fine_term[me]
 
     relay(2, middle_term, middle_parts, middle_send_on, middle_recv_on, 0, near)
     for r in order:

time: 72.2 us -> 72.1 us (level)
  no operation moved by 1% of the time
where the time goes in v7:
time: 72.1 us; the launch traced here: 71.9 us
  Pallas kernels  71.2 us (99%)
    pallas_call x1, Pallas kernels, exchange(): pl.pallas_call(functools.partial(main_kernel, groups, members), out_shape...  67.7 us
    pallas_call x1, Pallas kernels, collect(): pl.pallas_call(collect_kernel, out_shape=tuple((jax.ShapeDtypeStruct(shap...  3.54 us

profile of v7, /device:TPU:0, one launch (start us, length us, event | category | flops | bytes accessed | tf_op | source)
XLA Modules:
  0.0 71.9 jit_solution(811325662844539282)
XLA Ops:
  0.6 67.7 %exchange.1 = (s32[32,1,3]{2,1,0:T(1,128)}, bf16[128,1024]{1,0:T(8,128)(2,1)}, bf16[2,16,64,256]{3,2,1,0:T(8,128)(2,1)}, bf16[2,16,64,128]{3,2,1,0:T(8,128)(2,1)}, bf16[2,4,64,256]{3,2,1,0:T(8,128)(2,1)}) custom-call(s32[1,3]{1,0:T(1,128)} %path_row.1, bf16[128,1024]{1,0:T(8,128)(2,1)} %tokens_hbm.1, bf16[128,1024]{1,0:T(8,128)(2,1)} %cotangent_hbm.1, ...), custom_call_target="tpu_custom_call" | custom-call | tf_op jit(solution)/shard_map/exchange/pallas_call | solution.py:684
  68.3 3.5 %collect.1 = (bf16[128,1024]{1,0:T(8,128)(2,1)}, bf16[4,64,512]{2,1,0:T(8,128)(2,1)}, bf16[64,64,256]{2,1,0:T(8,128)(2,1)}, bf16[32,64,128]{2,1,0:T(8,128)(2,1)}) custom-call(s32[32,1,3]{2,1,0:T(1,128)} %get-tuple-element.9.path_hbm, bf16[128,1024]{1,0:T(8,128)(2,1)} %get-tuple-element.10.tokens_hbm, bf16[32,64,256]{2,1,0:T(8,128)(2,1)} %bitcast.2, ...), custom_call_target="tpu_custom_call" | custom-call | tf_op jit(solution)/shard_map/collect/pallas_call | solution.py:871

commit v8 on v7

--- a/solution.py
+++ b/solution.py
@@ -597,7 +597,7 @@
         if r:
             sums[flip(r), core] = folded(r).astype(BF16)
             fold_line(r, r & -r).start()
-            if r == 1:
+            if r == order[0]:
                 relay(2, middle_term, middle_parts, middle_send_on, middle_recv_on, near, members)
             if r == order[-2]:
                 relay(3, fine_term, fine_parts, fine_send_on, fine_recv_on)

time: 72.1 us -> 72.4 us (level)
  no operation moved by 1% of the time
where the time goes in v8:
time: 72.4 us; the launch traced here: 72.2 us
  Pallas kernels  71.5 us (99%)
    pallas_call x1, Pallas kernels, exchange(): pl.pallas_call(functools.partial(main_kernel, groups, members), out_shape...  68 us
    pallas_call x1, Pallas kernels, collect(): pl.pallas_call(collect_kernel, out_shape=tuple((jax.ShapeDtypeStruct(shap...  3.54 us

profile of v8, /device:TPU:0, one launch (start us, length us, event | category | flops | bytes accessed | tf_op | source)
XLA Modules:
  0.0 72.2 jit_solution(2070427753708697585)
XLA Ops:
  0.6 68.0 %exchange.1 = (s32[32,1,3]{2,1,0:T(1,128)}, bf16[128,1024]{1,0:T(8,128)(2,1)}, bf16[2,16,64,256]{3,2,1,0:T(8,128)(2,1)}, bf16[2,16,64,128]{3,2,1,0:T(8,128)(2,1)}, bf16[2,4,64,256]{3,2,1,0:T(8,128)(2,1)}) custom-call(s32[1,3]{1,0:T(1,128)} %path_row.1, bf16[128,1024]{1,0:T(8,128)(2,1)} %tokens_hbm.1, bf16[128,1024]{1,0:T(8,128)(2,1)} %cotangent_hbm.1, ...), custom_call_target="tpu_custom_call" | custom-call | tf_op jit(solution)/shard_map/exchange/pallas_call | solution.py:684
  68.6 3.5 %collect.1 = (bf16[128,1024]{1,0:T(8,128)(2,1)}, bf16[4,64,512]{2,1,0:T(8,128)(2,1)}, bf16[64,64,256]{2,1,0:T(8,128)(2,1)}, bf16[32,64,128]{2,1,0:T(8,128)(2,1)}) custom-call(s32[32,1,3]{2,1,0:T(1,128)} %get-tuple-element.9.path_hbm, bf16[128,1024]{1,0:T(8,128)(2,1)} %get-tuple-element.10.tokens_hbm, bf16[32,64,256]{2,1,0:T(8,128)(2,1)} %bitcast.2, ...), custom_call_target="tpu_custom_call" | custom-call | tf_op jit(solution)/shard_map/collect/pallas_call | solution.py:871
